TPU v7x, 16 devices: a 4x2x1 block of a 4x4x8 slice. The times are simulated.
16 devices in a mesh: rep: 2 (over y, z), dp: 8 (over x, core).
Axes of the slice: x: 4, y: 2, z: 1, core: 2. Of those that a mesh axis runs over, the one named last changes fastest.
The devices are a block of a 4x4x8 slice.
Arguments:
- g_w_gate: bfloat16 [16, 2, 896, 2560], P(('rep', 'dp')), parts along dimension 0
- g_w_up: bfloat16 [16, 2, 896, 2560], P(('rep', 'dp')), parts along dimension 0
- g_w_down: bfloat16 [16, 2, 2560, 896], P(('rep', 'dp')), parts along dimension 0
- w_gate: bfloat16 [2, 896, 2560], replicated
- w_up: bfloat16 [2, 896, 2560], replicated
- w_down: bfloat16 [2, 2560, 896], replicated
- m_w_gate: float32 [2, 896, 2560], P(None, 'dp')
- m_w_up: float32 [2, 896, 2560], P(None, 'dp')
- m_w_down: float32 [2, 2560, 896], P(None, 'dp')
- v_w_gate: float32 [2, 896, 2560], P(None, 'dp')
- v_w_up: float32 [2, 896, 2560], P(None, 'dp')
- v_w_down: float32 [2, 2560, 896], P(None, 'dp')
Outputs:
- output 1: bfloat16 [4, 896, 2560], P('rep'), parts along dimension 0
- output 2: bfloat16 [4, 896, 2560], P('rep'), parts along dimension 0
- output 3: bfloat16 [4, 2560, 896], P('rep'), parts along dimension 0
- output 4: float32 [4, 896, 2560], P('rep', 'dp'), parts along dimension 0
- output 5: float32 [4, 896, 2560], P('rep', 'dp'), parts along dimension 0
- output 6: float32 [4, 2560, 896], P('rep', 'dp'), parts along dimension 0
- output 7: float32 [4, 896, 2560], P('rep', 'dp'), parts along dimension 0
- output 8: float32 [4, 896, 2560], P('rep', 'dp'), parts along dimension 0
- output 9: float32 [4, 2560, 896], P('rep', 'dp'), parts along dimension 0
There are 2 independent parts. A program takes and returns all parts, laid end to end along the dimension named above; an argument that names none is the same for every part.
All inputs are finite; a program needn't handle non-finite values.
Results may differ from a plain program's by a relative error of at most 0.022.
Values are sent between devices in bfloat16 or wider.
A program may use at most 768 MiB of HBM per device.

v0:
```python
import jax
import jax.numpy as jnp
from jax import lax
from jax.sharding import PartitionSpec as P


def adamw(w, m, v, g):
    m = 0.9 * m + 0.1 * g
    v = 0.95 * v + 0.05 * g * g
    step = m * lax.rsqrt(v + 1e-8) + 0.1 * w
    return (w - 0.02 * step).astype(jnp.bfloat16), m, v


def clipped(gradients, sum_of_squares, count):
    factor = jnp.minimum(1.0, 0.5 * lax.rsqrt(sum_of_squares / count + 1e-30))
    return [g * factor for g in gradients]


def solution(mesh):
    def step(*arrays):
        terms, weights, m, v = (arrays[i : i + 3] for i in (0, 3, 6, 9))
        gradients = [lax.psum_scatter(t[0], "dp", scatter_dimension=1, tiled=True).astype(jnp.float32) for t in terms]
        squares = lax.psum(sum(jnp.sum(g * g) for g in gradients), "dp")
        gradients = clipped(gradients, squares, lax.psum(1, "dp") * sum(g.size for g in gradients))
        me = lax.axis_index("dp")
        own = [lax.dynamic_slice_in_dim(w, me * one.shape[1], one.shape[1], 1).astype(jnp.float32) for w, one in zip(weights, m, strict=True)]
        new = [adamw(w, m, v, g) for w, m, v, g in zip(own, m, v, gradients, strict=True)]
        whole = [lax.all_gather(one[0], "dp", axis=1, tiled=True) for one in new]
        return (*whole, *(one[1] for one in new), *(one[2] for one in new))

    all_of, cut = P(None, None, None), P(None, "dp", None)
    return jax.shard_map(
        step,
        mesh=mesh,
        in_specs=(P(("rep", "dp"), None, None, None),) * 3 + (all_of,) * 3 + (cut,) * 6,
        out_specs=(P("rep", None, None),) * 3 + (P("rep", "dp", None),) * 6,
        check_vma=False,
    )
```

profile of v0, /device:TPU:113, one launch (start us, length us, event | category | flops | bytes accessed | tf_op | source)
XLA Modules:
  0.0 378.2 jit_solution(6883706396897583059)
XLA Ops:
  7.2 0.1 reduce-scatter.4.cloned.1.call-start
  7.3 0.7 reduce-scatter.4.cloned.1.call-update
  8.0 0.1 reduce-scatter.6.cloned.1.call-start
  8.1 0.7 reduce-scatter.6.cloned.1.call-update
  8.8 0.1 reduce-scatter.8.cloned.1.call-start
  8.9 0.7 reduce-scatter.8.cloned.1.call-update
  9.6 0.1 all-gather.8.cloned.1.call-start
  9.7 55.3 %reduce-scatter.4.cloned.1.call-done = bf16[2,112,2560]{2,1,0:T(8,128)(2,1)} async-done(((bf16[2,896,2560]{2,1,0:T(8,128)(2,1)}), bf16[2,112,2560]{2,1,0:T(8,128)(2,1)}) %reduce-scatter.4.cloned.1.call-update) | async-done | bytes 1146896 | tf_op jit(solution)/shard_map/reduce_scatter | solution.py:22
  65.0 2.5 fusion.9
  67.4 51.7 %reduce-scatter.6.cloned.1.call-done = bf16[2,112,2560]{2,1,0:T(8,128)(2,1)} async-done(((bf16[2,896,2560]{2,1,0:T(8,128)(2,1)}), bf16[2,112,2560]{2,1,0:T(8,128)(2,1)}) %reduce-scatter.6.cloned.1.call-update) | async-done | bytes 1146896 | tf_op jit(solution)/shard_map/reduce_scatter | solution.py:22
  119.2 2.5 fusion.10
  122.9 50.4 %reduce-scatter.8.cloned.1.call-done = bf16[2,320,896]{2,1,0:T(8,128)(2,1)} async-done(((bf16[2,2560,896]{2,1,0:T(8,128)(2,1)}), bf16[2,320,896]{2,1,0:T(8,128)(2,1)}) %reduce-scatter.8.cloned.1.call-update) | async-done | bytes 1146896 | tf_op jit(solution)/shard_map/reduce_scatter | solution.py:22
  173.4 2.5 fusion.11
  176.5 13.4 %psum.7 = f32[]{:T(128)} all-reduce(f32[]{:T(128)S(6)} %add.65), channel_id=1, replica_groups=mesh['rep'=2,'dp'=8] {'dp'}, use_global_device_ids=true, to_apply=%region_6.0 | all-reduce | flops 1 | bytes 8 | tf_op jit(solution)/shard_map/psum | solution.py:23
  190.6 0.0 copy-start.1
  190.6 6.3 %fusion.17 = (bf16[2,320,896]{2,1,0:T(8,128)(2,1)}, f32[2,320,896]{2,1,0:T(8,128)}, f32[2,320,896]{2,1,0:T(8,128)}) fusion(bf16[2,2560,896]{2,1,0:T(8,128)(2,1)} %param.17, s32[]{:T(128)S(6)} %select_n.8, f32[]{:T(128)S(6)} %min_shard_map.3, bf16[2,320,896]{2,1,0:T(8,128)(2,1)} %reduce-scatter.8.cloned.1.call-done, f32[2,320,896]{2,1,0:T(8,128)} %param.23, ...), kind=kLoop, calls=%fused_computation.32 | loop fusion | flops 9748480 | bytes 12615688 | tf_op jit(solution)/shard_map/convert_element_type | solution.py:11
  196.9 0.1 all-gather.8.cloned.1.call-update
  196.9 0.1 all-gather.4.cloned.1.call-start
  197.0 0.0 copy-done.1
  197.0 0.0 copy-start
  197.0 6.0 %fusion.8 = (bf16[2,112,2560]{2,1,0:T(8,128)(2,1)}, f32[2,112,2560]{2,1,0:T(8,128)}, f32[2,112,2560]{2,1,0:T(8,128)}) fusion(bf16[2,896,2560]{2,1,0:T(8,128)(2,1)} %param.15, s32[]{:T(128)S(6)} %select_n.7, f32[]{:T(128)S(6)} %min_shard_map.3, bf16[2,112,2560]{2,1,0:T(8,128)(2,1)S(1)} %copy-done.1, f32[2,112,2560]{2,1,0:T(8,128)} %param.21, ...), kind=kLoop, calls=%fused_computation.23 | loop fusion | flops 9748480 | bytes 12615688 | tf_op jit(solution)/shard_map/convert_element_type | solution.py:11
  203.0 0.1 all-gather.4.cloned.1.call-update
  203.0 0.1 all-gather.6.cloned.1.call-start
  203.1 0.0 copy-done
  203.1 5.9 %fusion.14 = (bf16[2,112,2560]{2,1,0:T(8,128)(2,1)}, f32[2,112,2560]{2,1,0:T(8,128)}, f32[2,112,2560]{2,1,0:T(8,128)}) fusion(bf16[2,896,2560]{2,1,0:T(8,128)(2,1)} %param.16, s32[]{:T(128)S(6)} %select_n.7, f32[]{:T(128)S(6)} %min_shard_map.3, bf16[2,112,2560]{2,1,0:T(8,128)(2,1)S(1)} %copy-done, f32[2,112,2560]{2,1,0:T(8,128)} %param.22, ...), kind=kLoop, calls=%fused_computation.29 | loop fusion | flops 9748480 | bytes 12615688 | tf_op jit(solution)/shard_map/convert_element_type | solution.py:11
  209.0 0.1 all-gather.6.cloned.1.call-update
  209.1 36.4 %all-gather.8.cloned.1.call-done = bf16[2,2560,896]{2,1,0:T(8,128)(2,1)} async-done(((bf16[2,320,896]{2,1,0:T(8,128)(2,1)}), bf16[2,2560,896]{2,1,0:T(8,128)(2,1)}) %all-gather.8.cloned.1.call-update) | async-done | bytes 9175056 | tf_op jit(solution)/shard_map/all_gather | solution.py:28
  245.5 51.1 %all-gather.4.cloned.1.call-done = bf16[2,896,2560]{2,1,0:T(8,128)(2,1)} async-done(((bf16[2,112,2560]{2,1,0:T(8,128)(2,1)}), bf16[2,896,2560]{2,1,0:T(8,128)(2,1)}) %all-gather.4.cloned.1.call-update) | async-done | bytes 9175056 | tf_op jit(solution)/shard_map/all_gather | solution.py:28
  296.6 51.1 %all-gather.6.cloned.1.call-done = bf16[2,896,2560]{2,1,0:T(8,128)(2,1)} async-done(((bf16[2,112,2560]{2,1,0:T(8,128)(2,1)}), bf16[2,896,2560]{2,1,0:T(8,128)(2,1)}) %all-gather.6.cloned.1.call-update) | async-done | bytes 9175056 | tf_op jit(solution)/shard_map/all_gather | solution.py:28
  347.6 7.8 %copy.24 = bf16[2,896,2560]{2,1,0:T(8,128)(2,1)} copy(bf16[2,896,2560]{2,1,0:T(8,128)(2,1)} %all-gather.4.cloned.1.call-done) | data formatting | bytes 18350080
  355.5 7.9 %copy.25 = bf16[2,896,2560]{2,1,0:T(8,128)(2,1)} copy(bf16[2,896,2560]{2,1,0:T(8,128)(2,1)} %all-gather.6.cloned.1.call-done) | data formatting | bytes 18350080
  363.3 8.0 %copy.26 = bf16[2,2560,896]{2,1,0:T(8,128)(2,1)} copy(bf16[2,2560,896]{2,1,0:T(8,128)(2,1)} %all-gather.8.cloned.1.call-done) | data formatting | bytes 18350080
Async XLA Ops:
  7.2 57.8 %reduce-scatter.4.cloned.1.call-start = ((), (), s32[]{:S(2)}) async-start(), calls=%async_computation.3 | async-start | bytes 10321920 | tf_op jit(solution)/shard_map/reduce_scatter | solution.py:22
  8.0 111.2 %reduce-scatter.6.cloned.1.call-start = ((), (), s32[]{:S(2)}) async-start(), calls=%async_computation.4 | async-start | bytes 10321920 | tf_op jit(solution)/shard_map/reduce_scatter | solution.py:22
  8.8 164.6 %reduce-scatter.8.cloned.1.call-start = ((), (), s32[]{:S(2)}) async-start(), calls=%async_computation.5 | async-start | bytes 10321920 | tf_op jit(solution)/shard_map/reduce_scatter | solution.py:22
  9.6 235.9 %all-gather.8.cloned.1.call-start = ((), (), s32[]{:S(2)}) async-start(), calls=%async_computation.8 | async-start | bytes 10321920 | tf_op jit(solution)/shard_map/all_gather | solution.py:28
  190.6 6.4 %copy-start.1 = (bf16[2,112,2560]{2,1,0:T(8,128)(2,1)S(1)}, bf16[2,112,2560]{2,1,0:T(8,128)(2,1)}, u32[]{:S(2)}) copy-start(bf16[2,112,2560]{2,1,0:T(8,128)(2,1)} %reduce-scatter.4.cloned.1.call-done) | copy-start | bytes 3440644
  196.9 99.6 %all-gather.4.cloned.1.call-start = ((), (), s32[]{:S(2)}) async-start(), calls=%async_computation.6 | async-start | bytes 10321920 | tf_op jit(solution)/shard_map/all_gather | solution.py:28
  197.0 6.1 %copy-start = (bf16[2,112,2560]{2,1,0:T(8,128)(2,1)S(1)}, bf16[2,112,2560]{2,1,0:T(8,128)(2,1)}, u32[]{:S(2)}) copy-start(bf16[2,112,2560]{2,1,0:T(8,128)(2,1)} %reduce-scatter.6.cloned.1.call-done) | copy-start | bytes 3440644
  203.0 144.6 %all-gather.6.cloned.1.call-start = ((), (), s32[]{:S(2)}) async-start(), calls=%async_computation.7 | async-start | bytes 10321920 | tf_op jit(solution)/shard_map/all_gather | solution.py:28
Sparse Core Ops, SparseCore 0:
  10.3 54.6 reduce-scatter.3
  67.3 51.8 reduce-scatter.5
  121.5 51.8 reduce-scatter.7
  197.0 48.4 all-gather.7
  247.5 49.0 all-gather.3
  298.6 49.0 all-gather.5
where the time goes:
time: 379 us; the launch traced here: 378 us
  waiting for transfers between devices  298 us (79%)
  other arithmetic  25.5 us (7%)
  local copies, waits for them, and re-layouts  23.7 us (6%)
  between operations  16.8 us (4%)
  blocking collectives  13.4 us (4%)
    reduce_scatter x3, waiting for transfers between devices, step(): lax.psum_scatter(t[0], 'dp', scatter_dimension=1, tiled=True)  157 us
    all_gather x3, waiting for transfers between devices, step(): whole = [lax.all_gather(one[0], 'dp', axis=1, tiled=True) for one in new]  139 us
    unnamed x7, local copies, waits for them, and re-layouts  23.7 us
    convert_element_type x3, other arithmetic, adamw(): return ((w - 0.02 * step).astype(jnp.bfloat16), m, v)  18.2 us
    psum x1, blocking collectives, step(): squares = lax.psum(sum((jnp.sum(g * g) for g in gradients)), 'dp')  13.4 us
  transfers between devices with their start and end apart: 6, of which 6 were waited for; matrix products, arithmetic and copies ran while one was open for 4% of the time, Pallas kernels for 0%

commit v1 on v0

v1 whole, which is shorter than its diff:
```python
import functools

import jax
import jax.numpy as jnp
from jax import lax
from jax.experimental import pallas as pl
from jax.experimental.pallas import tpu as pltpu
from jax.sharding import PartitionSpec as P

MESH = pl.DeviceIdType.MESH
ROWS = 16
F32, BF16 = jnp.float32, jnp.bfloat16
LAYERS = (0, 1)


def chunks_of(units):
    gate, up, down = units
    a, b = gate // 7, 3 * gate // 7
    c, d, e = 12 * down // 20, 17 * down // 20, 19 * down // 20
    return [(0, 0, a), (0, a, b - a), (0, b, gate - b), (1, 0, up), (2, 0, c), (2, c, d - c), (2, d, e - d), (2, e, down - e)]


def kernel(n, count, chunks, *refs):
    g, w, m_in, v_in = refs[0:3], refs[3:6], refs[6:9], refs[9:12]
    new, m, v = refs[12:15], refs[15:18], refs[18:21]
    own, old = refs[21:24], refs[24:27]
    total, squares = refs[27:29]
    (d2d_send, d2d_recv, ici_send, ici_recv, load_sem, state_sem, sq_send, sq_recv) = refs[29:]

    me = lax.axis_index("dp")
    chip, core = me // 2, me % 2
    chips = n // 2
    partner = chip * 2 + 1 - core
    down_, up_, far = (chip + chips - 1) % chips, (chip + 1) % chips, (chip + 2) % chips
    sides = (down_, up_)

    def at(c):
        return c * 2 + core

    def remote(src, dst, send, recv, to):
        return pltpu.make_async_remote_copy(src_ref=src, dst_ref=dst, send_sem=send, recv_sem=recv, device_id={"dp": to}, device_id_type=MESH)

    blocks = ((far, far), (up_, down_), (down_, up_), (chip, chip))
    target = ((down_, up_), (up_, down_), (down_, up_))

    def load(p, l, t):
        return pltpu.make_async_copy(g[t].at[l, at(blocks[p][l])], own[t].at[l], load_sem.at[l, t])

    def state():
        return [
            copy
            for t in range(3)
            for copy in (
                pltpu.make_async_copy(w[t].at[:, me], old[t], state_sem.at[0, t]),
                pltpu.make_async_copy(m_in[t], m[t], state_sem.at[1, t]),
                pltpu.make_async_copy(v_in[t], v[t], state_sem.at[2, t]),
            )
        ]

    for t in range(3):
        for l in LAYERS:
            load(0, l, t).start()

    barrier = pltpu.get_barrier_semaphore()
    for k in range(1, n):
        pl.semaphore_signal(barrier, inc=1, device_id={"dp": (me + k) % n}, device_id_type=MESH)
    pl.semaphore_wait(barrier, n - 1)

    def handed(p, l, i):
        t, s, size = chunks[i]
        there = blocks[p][l] * 2 + 1 - core
        part = (l, there, pl.ds(s, size))
        return remote(g[t].at[part], new[t].at[part], d2d_send.at[p, l, i], d2d_recv.at[p, l, i], partner)

    for p in range(4):
        for i in range(len(chunks)):
            for l in LAYERS:
                handed(p, l, i).start()

    def inbox(j):
        return j * 2 + 1 - core

    def passed(p, l, i):
        t, s, size = chunks[i]
        return remote(
            new[t].at[l, at(blocks[p][l]), pl.ds(s, size)],
            new[t].at[l, inbox(p), pl.ds(s, size)],
            ici_send.at[p, l, i],
            ici_recv.at[p, l, i],
            at(target[p][l]),
        )

    total[...] = jnp.zeros_like(total)

    def add(p, l, i):
        t, s, size = chunks[i]
        block = at(blocks[p][l])

        @pl.loop(s, s + size)
        def _(r):
            x = own[t][l, r].astype(F32) + new[t][l, block, r].astype(F32)
            if p == 2:
                x = x + new[t][l, inbox(0), r].astype(F32)
            if p == 3:
                x = x + new[t][l, inbox(1), r].astype(F32) + new[t][l, inbox(2), r].astype(F32)
            x = x.astype(BF16)
            new[t][l, block, r] = x
            if p == 3:
                x = x.astype(F32)
                x = x * x
                parts = [x[:, k : k + 128] for k in range(0, x.shape[1], 128)]
                while len(parts) > 1:
                    parts = [a + b for a, b in zip(parts[::2], parts[1::2])] + ([parts[-1]] if len(parts) % 2 else [])
                total[...] += parts[0]

    for p in range(4):
        for i, (t, s, size) in enumerate(chunks):
            for l in LAYERS:
                if s == 0:
                    load(p, l, t).wait()
                handed(p, l, i).wait_recv()
                if p == 2:
                    passed(0, l, i).wait_recv()
                if p == 3:
                    passed(1, l, i).wait_recv()
                    passed(2, l, i).wait_recv()
                add(p, l, i)
                if p < 3:
                    passed(p, l, i).start()
                    if s + size == g[t].shape[2]:
                        load(p + 1, l, t).start()
        if p == 2:
            for copy in state():
                copy.start()

    for p in range(4):
        for i in range(len(chunks)):
            for l in LAYERS:
                handed(p, l, i).wait_send()
                if p < 3:
                    passed(p, l, i).wait_send()

    def told(k):
        return remote(squares.at[me], squares.at[me], sq_send.at[k], sq_recv.at[k], (me + k) % n)

    squares[me] = total[...]
    for k in range(1, n):
        told(k).start()
    for copy in state():
        copy.wait()
    for k in range(1, n):
        told(k).wait_recv()
    everything = squares[0]
    for k in range(1, n):
        everything = everything + squares[k]
    everything = jnp.sum(everything, axis=(0, 1), keepdims=True)
    factor = jnp.minimum(1.0, 0.5 * lax.rsqrt(everything / count + 1e-30))

    def spread(q, l, i):
        t, s, size = chunks[i]
        block = (chip, chip, sides[l])[q]
        part = (l, at(block), pl.ds(s, size))
        to = (sides[1 - l], sides[l], sides[1 - l])[q]
        return remote(new[t].at[part], new[t].at[part], ici_send.at[q, l, i], ici_recv.at[q, l, i], at(to))

    def came(q, l):
        return (sides[l], sides[1 - l], far)[q]

    def share(q, l, i):
        t, s, size = chunks[i]
        block = chip if q == 0 else came(q - 1, l)
        part = (l, at(block), pl.ds(s, size))
        return remote(new[t].at[part], new[t].at[part], d2d_send.at[q, l, i], d2d_recv.at[q, l, i], partner)

    for i, (t, s, size) in enumerate(chunks):
        for l in LAYERS:

            @pl.loop(s, s + size)
            def _(r, t=t, l=l):
                grad = new[t][l, me, r].astype(F32) * factor
                m1 = 0.9 * m[t][l, r] + 0.1 * grad
                v1 = 0.95 * v[t][l, r] + 0.05 * grad * grad
                w0 = old[t][l, r].astype(F32)
                step = m1 * lax.rsqrt(v1 + 1e-8) + 0.1 * w0
                new[t][l, me, r] = (w0 - 0.02 * step).astype(BF16)
                m[t][l, r] = m1
                v[t][l, r] = v1

            spread(0, l, i).start()
            share(0, l, i).start()
    for i in range(len(chunks)):
        for l in LAYERS:
            spread(1, l, i).start()
    for q in range(3):
        for i in range(len(chunks)):
            for l in LAYERS:
                spread(q, l, i).wait_recv()
                if q == 0:
                    spread(2, l, i).start()
                share(q + 1, l, i).start()
    for q in range(4):
        for i in range(len(chunks)):
            for l in LAYERS:
                share(q, l, i).wait_recv()
    for q in range(4):
        for i in range(len(chunks)):
            for l in LAYERS:
                share(q, l, i).wait_send()
                if q < 3:
                    spread(q, l, i).wait_send()
    for k in range(1, n):
        told(k).wait_send()


def put_out(*refs):
    copies = [pltpu.make_async_copy(refs[i], refs[9 + i], refs[18].at[i]) for i in range(9)]
    for copy in copies:
        copy.start()
    for copy in copies:
        copy.wait()


OUT = pltpu.VMEM


def solution(mesh):
    n = mesh.shape["dp"]

    def step(*arrays):
        terms, weights, ms, vs = (arrays[i : i + 3] for i in (0, 3, 6, 9))
        layers = weights[0].shape[0]
        units = [one.shape[1] // ROWS for one in ms]
        cols = [one.shape[2] for one in ms]
        chunks = chunks_of(units)
        count = n * sum(one.size for one in ms)
        whole = [(layers, n, u, ROWS, c) for u, c in zip(units, cols)]
        part = [(layers, u, ROWS, c) for u, c in zip(units, cols)]
        operands = (
            [t.reshape(s) for t, s in zip(terms, whole)]
            + [x.reshape(s) for x, s in zip(weights, whole)]
            + [x.reshape(s) for x, s in zip(ms, part)]
            + [x.reshape(s) for x, s in zip(vs, part)]
        )
        k = len(chunks)
        dma = pltpu.SemaphoreType.DMA
        outs = pl.pallas_call(
            functools.partial(kernel, n, count, chunks),
            name="step",
            out_shape=[OUT(s, BF16) for s in whole] + [OUT(s, F32) for s in part] * 2,
            in_specs=[pl.BlockSpec(memory_space=pltpu.HBM)] * 12,
            out_specs=[pl.BlockSpec(memory_space=OUT)] * 9,
            scratch_shapes=[pltpu.VMEM((2, *s[1:]), BF16) for s in part]
            + [pltpu.VMEM(s, BF16) for s in part]
            + [pltpu.VMEM((ROWS, 128), F32), pltpu.VMEM((n, ROWS, 128), F32)]
            + [dma((4, 2, k)), dma((4, 2, k)), dma((3, 2, k)), dma((3, 2, k)), dma((2, 3)), dma((3, 3)), dma((n,)), dma((n,))],
            compiler_params=pltpu.CompilerParams(collective_id=0, has_side_effects=True, vmem_limit_bytes=LIMIT),
        )(*[pltpu.with_memory_space_constraint(o, pltpu.HBM) for o in operands])
        outs = pl.pallas_call(
            put_out,
            name="put_out",
            out_shape=[pltpu.HBM(s, BF16) for s in whole] + [pltpu.HBM(s, F32) for s in part] * 2,
            in_specs=[pl.BlockSpec(memory_space=OUT)] * 9,
            out_specs=[pl.BlockSpec(memory_space=pltpu.HBM)] * 9,
            scratch_shapes=[dma((9,))],
            compiler_params=pltpu.CompilerParams(has_side_effects=True, vmem_limit_bytes=2**20),
        )(*outs)
        shapes = [x.shape for x in weights] + [x.shape for x in ms] * 2
        return tuple(o.reshape(s) for o, s in zip(outs, shapes))

    all_of, cut = P(None, None, None), P(None, "dp", None)
    return jax.shard_map(
        step,
        mesh=mesh,
        in_specs=(P(("rep", "dp"), None, None, None),) * 3 + (all_of,) * 3 + (cut,) * 6,
        out_specs=(P("rep", None, None),) * 3 + (P("rep", "dp", None),) * 6,
        check_vma=False,
    )


LIMIT = 8 * 2**20
```

time: 379 us -> 254 us (0.67)
  waiting for transfers between devices: 298 us -> 0 us
  Pallas kernels: 0 us -> 253 us
  other arithmetic: 25.5 us -> 0 us
  local copies, waits for them, and re-layouts: 23.7 us -> 0 us
  between operations: 16.8 us -> 0.65 us
  blocking collectives: 13.4 us -> 0 us
    pallas_call x0 -> x2, Pallas kernels: none -> 253 us  [the longest x1 239 us: step(): pl.pallas_call(functools.partial(kernel, n, count, chunks), name='step',...]
    reduce_scatter x3 -> x0, waiting for transfers between devices: 157 us -> none  [step(): lax.psum_scatter(t[0], 'dp', scatter_dimension=1, tiled=True)]
    all_gather x3 -> x0, waiting for transfers between devices: 139 us -> none  [step(): whole = [lax.all_gather(one[0], 'dp', axis=1, tiled=True) for one in new]]
    unnamed x7 -> x0, local copies, waits for them, and re-layouts: 23.7 us -> none
    convert_element_type x3 -> x0, other arithmetic: 18.2 us -> none  [adamw(): return ((w - 0.02 * step).astype(jnp.bfloat16), m, v)]
    psum x1 -> x0, blocking collectives: 13.4 us -> none  [step(): squares = lax.psum(sum((jnp.sum(g * g) for g in gradients)), 'dp')]
    reduce_sum x3 -> x0, other arithmetic: 7.36 us -> none  [step(): squares = lax.psum(sum((jnp.sum(g * g) for g in gradients)), 'dp')]
  transfers between devices with their start and end apart: 6 -> 0, of which waited for: 6 -> 0; matrix products, arithmetic and copies ran while one was open for 4% -> 0% of each run, Pallas kernels for 0% -> 0%
where the time goes in v1:
time: 254 us; the launch traced here: 253 us
  Pallas kernels  253 us (100%)
    pallas_call x1, Pallas kernels, step(): pl.pallas_call(functools.partial(kernel, n, count, chunks), name='step',...  239 us
    pallas_call x1, Pallas kernels, step(): pl.pallas_call(put_out, name='put_out', out_shape=[pltpu.HBM(s, BF16) for...  13.5 us

profile of v1, /device:TPU:113, one launch (start us, length us, event | category | flops | bytes accessed | tf_op | source)
XLA Modules:
  0.0 253.5 jit_solution(15260911680303981351)
XLA Ops:
  0.6 239.3 %step.1 = (bf16[2,8,7,16,2560]{4,3,2,1,0:T(8,128)(2,1)S(1)}, bf16[2,8,7,16,2560]{4,3,2,1,0:T(8,128)(2,1)S(1)}, bf16[2,8,20,16,896]{4,3,2,1,0:T(8,128)(2,1)S(1)},...) custom-call(bf16[2,8,7,16,2560]{4,3,2,1,0:T(8,128)(2,1)} %bitcast.21, ...), custom_call_target="tpu_custom_call" | custom-call | tf_op jit(solution)/shard_map/step/pallas_call | solution.py:246
  240.0 13.5 %put_out.1 = (bf16[2,8,7,16,2560]{4,3,2,1,0:T(8,128)(2,1)}, bf16[2,8,7,16,2560]{4,3,2,1,0:T(8,128)(2,1)}, bf16[2,8,20,16,896]{4,3,2,1,0:T(8,128)(2,1)}, f32[2,7,...) custom-call(bf16[2,8,7,16,2560]{4,3,2,1,0:T(8,128)(2,1)S(1)} %get-tu, ...), custom_call_target="tpu_custom_call" | custom-call | tf_op jit(solution)/shard_map/put_out/pallas_call | solution.py:258

commit v2 on v1

v2 whole, which is shorter than its diff:
```python
import functools

import jax
import jax.numpy as jnp
from jax import lax
from jax.experimental import pallas as pl
from jax.experimental.pallas import tpu as pltpu
from jax.sharding import PartitionSpec as P

MESH = pl.DeviceIdType.MESH
ROWS = 16
VMEM_LIMIT = 8 * 2**20
F32, BF16 = jnp.float32, jnp.bfloat16
LAYERS = (0, 1)


def chunks_of(units):
    gate, up, down = units
    a, b = gate // 7, 3 * gate // 7
    head = [(0, 0, a), (0, a, b - a), (0, b, gate - b)]
    c, d, e = 12 * down // 20, 17 * down // 20, 19 * down // 20
    sums = head + [(1, 0, up), (2, 0, c), (2, c, d - c), (2, d, e - d), (2, e, down - e)]
    c, d, e = down // 10, 3 * down // 20, down // 5
    news = head + [(2, e, down - e), (1, 0, up), (2, 0, c), (2, c, d - c), (2, d, e - d)]
    return sums, news


def kernel(n, count, sums, news, *refs):
    g, w, m_in, v_in = refs[0:3], refs[3:6], refs[6:9], refs[9:12]
    new, m, v = refs[12:15], refs[15:18], refs[18:21]
    piece = refs[21:23]
    own, old = refs[23:26], refs[26:29]
    total, squares = refs[29:31]
    (d2d_send, d2d_recv, ici_send, ici_recv, load_sem, state_sem, sq_send, sq_recv, piece_sem) = refs[31:]

    me = lax.axis_index("dp")
    chip, core = me // 2, me % 2
    chips = n // 2
    partner = chip * 2 + 1 - core
    down_, up_, far = (chip + chips - 1) % chips, (chip + 1) % chips, (chip + 2) % chips
    sides = (down_, up_)

    def at(c):
        return c * 2 + core

    def remote(src, dst, send, recv, to):
        return pltpu.make_async_remote_copy(src_ref=src, dst_ref=dst, send_sem=send, recv_sem=recv, device_id={"dp": to}, device_id_type=MESH)

    blocks = ((far, far), (up_, down_), (down_, up_), (chip, chip))
    target = ((down_, up_), (up_, down_), (down_, up_))

    def load(p, l, t):
        return pltpu.make_async_copy(g[t].at[l, at(blocks[p][l])], own[t].at[l], load_sem.at[l, t])

    def state():
        return [
            copy
            for t in range(3)
            for copy in (
                pltpu.make_async_copy(w[t].at[:, me], old[t], state_sem.at[0, t]),
                pltpu.make_async_copy(m_in[t], m[t], state_sem.at[1, t]),
                pltpu.make_async_copy(v_in[t], v[t], state_sem.at[2, t]),
            )
        ]

    for t in range(3):
        for l in LAYERS:
            load(0, l, t).start()

    barrier = pltpu.get_barrier_semaphore()
    for k in range(1, n):
        pl.semaphore_signal(barrier, inc=1, device_id={"dp": (me + k) % n}, device_id_type=MESH)
    pl.semaphore_wait(barrier, n - 1)

    def handed(p, l, i):
        t, s, size = sums[i]
        there = blocks[p][l] * 2 + 1 - core
        part = (l, there, pl.ds(s, size))
        return remote(g[t].at[part], new[t].at[part], d2d_send.at[0, t], d2d_recv.at[p, l, i], partner)

    for p in range(4):
        for i in range(len(sums)):
            for l in LAYERS:
                handed(p, l, i).start()

    def inbox(j):
        return j * 2 + 1 - core

    def passed(p, l, i):
        t, s, size = sums[i]
        return remote(
            new[t].at[l, at(blocks[p][l]), pl.ds(s, size)],
            new[t].at[l, inbox(p), pl.ds(s, size)],
            ici_send.at[0, t],
            ici_recv.at[p, l, i],
            at(target[p][l]),
        )

    total[...] = jnp.zeros_like(total)

    def add(p, l, i):
        t, s, size = sums[i]
        block = at(blocks[p][l])

        @pl.loop(s, s + size)
        def _(r):
            x = own[t][l, r].astype(F32) + new[t][l, block, r].astype(F32)
            if p == 2:
                x = x + new[t][l, inbox(0), r].astype(F32)
            if p == 3:
                x = x + new[t][l, inbox(1), r].astype(F32) + new[t][l, inbox(2), r].astype(F32)
            x = x.astype(BF16)
            new[t][l, block, r] = x
            if p == 3:
                x = x.astype(F32)
                x = x * x
                parts = [x[:, k : k + 128] for k in range(0, x.shape[1], 128)]
                while len(parts) > 1:
                    parts = [a + b for a, b in zip(parts[::2], parts[1::2])] + ([parts[-1]] if len(parts) % 2 else [])
                total[...] += parts[0]

    for p in range(4):
        for i, (t, s, size) in enumerate(sums):
            for l in LAYERS:
                if s == 0:
                    load(p, l, t).wait()
                handed(p, l, i).wait_recv()
                if p == 2:
                    passed(0, l, i).wait_recv()
                if p == 3:
                    passed(1, l, i).wait_recv()
                    passed(2, l, i).wait_recv()
                add(p, l, i)
                if p < 3:
                    passed(p, l, i).start()
                    if s + size == g[t].shape[2]:
                        load(p + 1, l, t).start()
        if p == 2:
            for copy in state():
                copy.start()

    def sent(t, blocks, sem):
        part = new[t].at[:, pl.ds(0, blocks)]
        pltpu.make_async_copy(part, part, sem).wait()

    for t in range(3):
        sent(t, 4, d2d_send.at[0, t])
        sent(t, 3, ici_send.at[0, t])

    def told(k):
        return remote(squares.at[me], squares.at[me], sq_send.at[k], sq_recv.at[k], (me + k) % n)

    squares[me] = jnp.sum(total[...], axis=0, keepdims=True)
    for k in range(1, n):
        told(k).start()
    for copy in state():
        copy.wait()
    for k in range(1, n):
        told(k).wait_recv()
    everything = squares[0]
    for k in range(1, n):
        everything = everything + squares[k]
    everything = jnp.sum(everything, axis=(0, 1), keepdims=True)
    factor = jnp.minimum(1.0, 0.5 * lax.rsqrt(everything / count + 1e-30))

    rest = news[3]

    def spread(q, l, i):
        t, s, size = news[i]
        block = (chip, chip, sides[l])[q]
        part = (l, at(block), pl.ds(s, size))
        to = (sides[1 - l], sides[l], sides[1 - l])[q]
        return remote(new[t].at[part], new[t].at[part], ici_send.at[q // 2, t], ici_recv.at[q, l, i], at(to))

    def came(q, l):
        return (sides[l], sides[1 - l], far)[q]

    def share(q, l, i):
        t, s, size = news[i]
        block = chip if q == 0 else came(q - 1, l)
        part = (l, at(block), pl.ds(s, size))
        arrived = d2d_recv.at[3, l, i] if q == 3 else d2d_recv.at[0, 0, t]
        return remote(new[t].at[part], new[t].at[part], d2d_send.at[q // 3, t], arrived, partner)

    def keep(l):
        t, s, size = rest
        return pltpu.make_async_copy(new[t].at[l, at(sides[l]), pl.ds(s, size)], piece[l], piece_sem.at[l])

    for i, (t, s, size) in enumerate(news):
        for l in LAYERS:

            @pl.loop(s, s + size)
            def _(r, t=t, l=l):
                grad = new[t][l, me, r].astype(F32) * factor
                m1 = 0.9 * m[t][l, r] + 0.1 * grad
                v1 = 0.95 * v[t][l, r] + 0.05 * grad * grad
                w0 = old[t][l, r].astype(F32)
                step = m1 * lax.rsqrt(v1 + 1e-8) + 0.1 * w0
                new[t][l, me, r] = (w0 - 0.02 * step).astype(BF16)
                m[t][l, r] = m1
                v[t][l, r] = v1

            spread(0, l, i).start()
            share(0, l, i).start()
    for i in range(len(news)):
        for l in LAYERS:
            spread(1, l, i).start()
    for k in range(1, n):
        told(k).wait_send()
    for q in range(3):
        for i in range(len(news)):
            for l in LAYERS:
                if q == 2 and news[i] == rest:
                    continue
                spread(q, l, i).wait_recv()
                if q == 0 and news[i] == rest:
                    keep(l).start()
                elif q == 0:
                    spread(2, l, i).start()
                share(q + 1, l, i).start()
        if q == 1:
            for l in LAYERS:
                keep(l).wait()
            for t in range(3):
                sent(t, 2, ici_send.at[0, t])
    for t in range(3):
        sent(t, 3, d2d_recv.at[0, 0, t])
        sent(t, 3, d2d_send.at[0, t])
    for i in range(len(news)):
        for l in LAYERS:
            if news[i] != rest:
                share(3, l, i).wait_recv()
    for t in range(3):
        units = rest[1] if t == rest[0] else new[t].shape[2]
        part = new[t].at[:, pl.ds(0, 1), pl.ds(0, units)]
        pltpu.make_async_copy(part, part, d2d_send.at[1, t]).wait()
        pltpu.make_async_copy(part, part, ici_send.at[1, t]).wait()


def put_out(k, *refs):
    copies = [pltpu.make_async_copy(refs[i], refs[k + i], refs[2 * k].at[i]) for i in range(k)]
    for copy in copies:
        copy.start()
    for copy in copies:
        copy.wait()


def written(name, *arrays):
    k = len(arrays)
    size = sum(a.size * a.dtype.itemsize for a in arrays)
    return pl.pallas_call(
        functools.partial(put_out, k),
        name=name,
        out_shape=[pltpu.HBM(a.shape, a.dtype) for a in arrays],
        in_specs=[IN_VMEM] * k,
        out_specs=[IN_HBM] * k,
        scratch_shapes=[pltpu.SemaphoreType.DMA((k,))],
        cost_estimate=pl.CostEstimate(flops=100 * size, bytes_accessed=size, transcendentals=0),
        compiler_params=pltpu.CompilerParams(has_side_effects=True, vmem_limit_bytes=VMEM_LIMIT),
    )(*arrays)


def patch(n, down, *refs):
    parts, out, sem = refs[:4], refs[4], refs[5]
    me = lax.axis_index("dp")
    far, core = (me // 2 + 2) % (n // 2), me % 2
    first = out.shape[2] - parts[0].shape[0]
    copies = []
    for i, part in enumerate(parts):
        block = far * 2 + (core if i < 2 else 1 - core)
        copies.append(pltpu.make_async_copy(part, out.at[i % 2, block, pl.ds(first, part.shape[0])], sem.at[i]))
    for copy in copies:
        copy.start()
    for copy in copies:
        copy.wait()


IN_VMEM, IN_HBM = pl.BlockSpec(memory_space=pltpu.VMEM), pl.BlockSpec(memory_space=pltpu.HBM)


def solution(mesh):
    n = mesh.shape["dp"]
    chips = n // 2
    ring = [(2 * c + k, 2 * ((c + 1) % chips) + k) for c in range(chips) for k in range(2)]
    back = [(b, a) for a, b in ring]
    swap = [(d, d + 1 - 2 * (d % 2)) for d in range(n)]

    def step(*arrays):
        terms, weights, ms, vs = (arrays[i : i + 3] for i in (0, 3, 6, 9))
        layers = weights[0].shape[0]
        units = [one.shape[1] // ROWS for one in ms]
        cols = [one.shape[2] for one in ms]
        sums, news = chunks_of(units)
        count = n * sum(one.size for one in ms)
        whole = [(layers, n, u, ROWS, c) for u, c in zip(units, cols)]
        part = [(layers, u, ROWS, c) for u, c in zip(units, cols)]
        left = (news[3][2], ROWS, cols[2])
        operands = (
            [t.reshape(s) for t, s in zip(terms, whole)]
            + [x.reshape(s) for x, s in zip(weights, whole)]
            + [x.reshape(s) for x, s in zip(ms, part)]
            + [x.reshape(s) for x, s in zip(vs, part)]
        )
        k = max(len(sums), len(news))
        dma = pltpu.SemaphoreType.DMA
        outs = pl.pallas_call(
            functools.partial(kernel, n, count, sums, news),
            name="step",
            out_shape=[pltpu.VMEM(s, BF16) for s in whole] + [pltpu.VMEM(s, F32) for s in part] * 2 + [pltpu.HBM(left, BF16)] * 2,
            in_specs=[IN_HBM] * 12,
            out_specs=[IN_VMEM] * 9 + [IN_HBM] * 2,
            scratch_shapes=[pltpu.VMEM((2, *s[1:]), BF16) for s in part]
            + [pltpu.VMEM(s, BF16) for s in part]
            + [pltpu.VMEM((ROWS, 128), F32), pltpu.VMEM((n, 1, 128), F32)]
            + [dma((2, 3)), dma((4, 2, k)), dma((2, 3)), dma((3, 2, k)), dma((2, 3)), dma((3, 3)), dma((n,)), dma((n,)), dma((2,))],
            compiler_params=pltpu.CompilerParams(collective_id=0, has_side_effects=True, vmem_limit_bytes=VMEM_LIMIT),
        )(*[pltpu.with_memory_space_constraint(o, pltpu.HBM) for o in operands])
        gate, up, down, *moments = outs[:9]
        over = [lax.ppermute(outs[9], "dp", ring), lax.ppermute(outs[10], "dp", back)]
        first = written("put_first", *moments, gate, up)
        over[0], over[1] = lax.optimization_barrier((*over, first[0]))[:2]
        across = [lax.ppermute(o, "dp", swap) for o in over]
        (last,) = written("put_last", down)
        new_down = pl.pallas_call(
            functools.partial(patch, n),
            name="patch",
            out_shape=pltpu.HBM(last.shape, BF16),
            in_specs=[IN_HBM] + [IN_VMEM] * 4,
            out_specs=IN_HBM,
            scratch_shapes=[dma((4,))],
            input_output_aliases={0: 0},
            compiler_params=pltpu.CompilerParams(has_side_effects=True, vmem_limit_bytes=VMEM_LIMIT),
        )(last, *[pltpu.with_memory_space_constraint(o, pltpu.VMEM) for o in over + across])
        outs = (first[6], first[7], new_down, *first[:6])
        shapes = [x.shape for x in weights] + [x.shape for x in ms] * 2
        return tuple(o.reshape(s) for o, s in zip(outs, shapes))

    all_of, cut = P(None, None, None), P(None, "dp", None)
    return jax.shard_map(
        step,
        mesh=mesh,
        in_specs=(P(("rep", "dp"), None, None, None),) * 3 + (all_of,) * 3 + (cut,) * 6,
        out_specs=(P("rep", None, None),) * 3 + (P("rep", "dp", None),) * 6,
        check_vma=False,
    )
```

time: 254 us -> 248 us (0.976)
  Pallas kernels: 253 us -> 244 us
  starting transfers between devices: 0 us -> 3.61 us
    pallas_call x2 -> x4, Pallas kernels: 253 us -> 244 us  [the longest x1 228 us: step(): pl.pallas_call(functools.partial(kernel, n, count, sums, news), name='ste...]
    ppermute x0 -> x4, starting transfers between devices: none -> 3.61 us  [the longest x1 2.53 us: step(): lax.ppermute(outs[10], 'dp', back)]
  transfers between devices with their start and end apart: 0 -> 4, of which waited for: 0 -> 0; matrix products, arithmetic and copies ran while one was open for 0% -> 0% of each run, Pallas kernels for 0% -> 6%
where the time goes in v2:
time: 248 us
  Pallas kernels  244 us (98%)
  starting transfers between devices  3.61 us (1%)
    pallas_call x1, Pallas kernels, step(): pl.pallas_call(functools.partial(kernel, n, count, sums, news), name='ste...  228 us
    pallas_call x2, Pallas kernels, written(): pl.pallas_call(functools.partial(put_out, k), name=name, out_shape=[pltpu...  14.4 us
  transfers between devices with their start and end apart: 4, of which 0 were waited for; matrix products, arithmetic and copies ran while one was open for 0% of the time, Pallas kernels for 6%

profile of v2, /device:TPU:113, one launch (start us, length us, event | category | flops | bytes accessed | tf_op | source)
XLA Modules:
  0.0 248.2 jit_solution(1375760709611789110)
XLA Ops:
  0.6 228.2 %step.1 = (bf16[2,8,7,16,2560]{4,3,2,1,0:T(8,128)(2,1)S(1)}, bf16[2,8,7,16,2560]{4,3,2,1,0:T(8,128)(2,1)S(1)}, bf16[2,8,20,16,896]{4,3,2,1,0:T(8,128)(2,1)S(1)},...) custom-call(bf16[2,8,7,16,2560]{4,3,2,1,0:T(8,128)(2,1)} %bitcast.22, ...), custom_call_target="tpu_custom_call" | custom-call | tf_op jit(solution)/shard_map/step/pallas_call | solution.py:306
  228.9 0.2 collective-permute-start
  229.1 2.5 %collective-permute-start.1 = (bf16[16,16,896]{2,1,0:T(8,128)(2,1)}, bf16[16,16,896]{2,1,0:T(8,128)(2,1)S(1)}, u32[]{:S(2)}, u32[]{:S(2)}) collective-permute-start(bf16[16,16,896]{2,1,0:T(8,128)(2,1)} %get-tuple-element.42), channel_id=1, source_target_pairs={{2,0},{3,1},{4,2},{5,3},{6,4},{7,5},{0,6},{1,7},{10,8},{11,9},{12,... | collective-permute-start | bytes 1376264 | tf_op jit(solution)/shard_map/ppermute | solution.py:319
  231.6 10.8 %put_first.1 = (f32[2,7,16,2560]{3,2,1,0:T(8,128)}, f32[2,7,16,2560]{3,2,1,0:T(8,128)}, f32[2,20,16,896]{3,2,1,0:T(8,128)}, f32[2,7,16,2560]{3,2,1,0:T(8,128)}, ...) custom-call(f32[2,7,16,2560]{3,2,1,0:T(8,128)S(1)} %get-tuple-elemen, ...), custom_call_target="tpu_custom_call" | custom-call | flops 3211264000 | bytes 32112640 | tf_op jit(solution)/shard_map/put_first/pallas_call | solution.py:251
  242.4 0.0 collective-permute-done.refs_0_
  242.4 0.0 collective-permute-done.1.refs_1_
  242.4 0.8 collective-permute-start.2
  243.2 0.1 collective-permute-start.3
  243.3 3.7 %put_last.1.down = bf16[2,8,20,16,896]{4,3,2,1,0:T(8,128)(2,1)} custom-call(bf16[2,8,20,16,896]{4,3,2,1,0:T(8,128)(2,1)S(1)} %get-tuple-element.40.refs_0_), custom_call_target="tpu_custom_call" | custom-call | flops 917504000 | bytes 9175040 | tf_op jit(solution)/shard_map/put_last/pallas_call | solution.py:251
  246.9 0.0 collective-permute-done.2.refs_2_
  246.9 0.0 collective-permute-done.3.refs_3_
  247.0 1.3 patch.1
Async XLA Ops:
  228.9 13.5 %collective-permute-start = (bf16[16,16,896]{2,1,0:T(8,128)(2,1)}, bf16[16,16,896]{2,1,0:T(8,128)(2,1)S(1)}, u32[]{:S(2)}, u32[]{:S(2)}) collective-permute-start(bf16[16,16,896]{2,1,0:T(8,128)(2,1)} %get-tuple-element.41), channel_id=1, source_target_pairs={{0,2},{1,3},{2,4},{3,5},{4,6},{5,7},{6,0},{7,1},{8,10},{9,11},{10,... | collective-permute-start | bytes 1376264 | tf_op jit(solution)/shard_map/ppermute | solution.py:319
  229.1 13.3 %collective-permute-start.1 = (bf16[16,16,896]{2,1,0:T(8,128)(2,1)}, bf16[16,16,896]{2,1,0:T(8,128)(2,1)S(1)}, u32[]{:S(2)}, u32[]{:S(2)}) collective-permute-start(bf16[16,16,896]{2,1,0:T(8,128)(2,1)} %get-tuple-element.42), channel_id=1, source_target_pairs={{2,0},{3,1},{4,2},{5,3},{6,4},{7,5},{0,6},{1,7},{10,8},{11,9},{12,... | collective-permute-start | bytes 1376264 | tf_op jit(solution)/shard_map/ppermute | solution.py:319
  242.4 4.5 %collective-permute-start.2 = (bf16[16,16,896]{2,1,0:T(8,128)(2,1)S(1)}, bf16[16,16,896]{2,1,0:T(8,128)(2,1)S(1)}, u32[]{:S(2)}, u32[]{:S(2)}) collective-permute-start(bf16[16,16,896]{2,1,0:T(8,128)(2,1)S(1)} %collective-permute-done.refs_0_), channel_id=1, source_target_pairs={{0,1},{1,0},{2,3},{3,2},{4,5},{5,4},{6,7},{7,6},{8,9},{9,8},{10,11... | collective-permute-start | bytes 1376264 | tf_op jit(solution)/shard_map/ppermute | solution.py:322
  243.2 3.8 %collective-permute-start.3 = (bf16[16,16,896]{2,1,0:T(8,128)(2,1)S(1)}, bf16[16,16,896]{2,1,0:T(8,128)(2,1)S(1)}, u32[]{:S(2)}, u32[]{:S(2)}) collective-permute-start(bf16[16,16,896]{2,1,0:T(8,128)(2,1)S(1)} %collective-permute-done.1.refs_1_), channel_id=1, source_target_pairs={{0,1},{1,0},{2,3},{3,2},{4,5},{5,4},{6,7},{7,6},{8,9},{9,8},{10,11... | collective-permute-start | bytes 1376264 | tf_op jit(solution)/shard_map/ppermute | solution.py:322

commit v3 on v2

--- a/solution.py
+++ b/solution.py
@@ -17,21 +17,18 @@
 def chunks_of(units):
     gate, up, down = units
     a, b = gate // 7, 3 * gate // 7
-    head = [(0, 0, a), (0, a, b - a), (0, b, gate - b)]
     c, d, e = 12 * down // 20, 17 * down // 20, 19 * down // 20
-    sums = head + [(1, 0, up), (2, 0, c), (2, c, d - c), (2, d, e - d), (2, e, down - e)]
-    c, d, e = down // 10, 3 * down // 20, down // 5
-    news = head + [(2, e, down - e), (1, 0, up), (2, 0, c), (2, c, d - c), (2, d, e - d)]
-    return sums, news
-
-
-def kernel(n, count, sums, news, *refs):
+    chunks = [(0, 0, a), (0, a, b - a), (0, b, gate - b), (1, 0, up), (2, 0, c), (2, c, d - c), (2, d, e - d), (2, e, down - e)]
+    return chunks, (1, 2, 3)
+
+
+def kernel(n, count, chunks, left, *refs):
     g, w, m_in, v_in = refs[0:3], refs[3:6], refs[6:9], refs[9:12]
     new, m, v = refs[12:15], refs[15:18], refs[18:21]
-    piece = refs[21:23]
-    own, old = refs[23:26], refs[26:29]
-    total, squares = refs[29:31]
-    (d2d_send, d2d_recv, ici_send, ici_recv, load_sem, state_sem, sq_send, sq_recv, piece_sem) = refs[31:]
+    piece = refs[21]
+    own, old = refs[22:25], refs[25:28]
+    total, squares = refs[28:30]
+    (d2d_send, d2d_recv, ici_send, ici_recv, load_sem, state_sem, sq_send, sq_recv) = refs[30:]
 
     me = lax.axis_index("dp")
     chip, core = me // 2, me % 2
@@ -73,13 +70,13 @@
     pl.semaphore_wait(barrier, n - 1)
 
     def handed(p, l, i):
-        t, s, size = sums[i]
+        t, s, size = chunks[i]
         there = blocks[p][l] * 2 + 1 - core
         part = (l, there, pl.ds(s, size))
         return remote(g[t].at[part], new[t].at[part], d2d_send.at[0, t], d2d_recv.at[p, l, i], partner)
 
     for p in range(4):
-        for i in range(len(sums)):
+        for i in range(len(chunks)):
             for l in LAYERS:
                 handed(p, l, i).start()
 
@@ -87,7 +84,7 @@
         return j * 2 + 1 - core
 
     def passed(p, l, i):
-        t, s, size = sums[i]
+        t, s, size = chunks[i]
         return remote(
             new[t].at[l, at(blocks[p][l]), pl.ds(s, size)],
             new[t].at[l, inbox(p), pl.ds(s, size)],
@@ -99,7 +96,7 @@
     total[...] = jnp.zeros_like(total)
 
     def add(p, l, i):
-        t, s, size = sums[i]
+        t, s, size = chunks[i]
         block = at(blocks[p][l])
 
         @pl.loop(s, s + size)
@@ -120,7 +117,7 @@
                 total[...] += parts[0]
 
     for p in range(4):
-        for i, (t, s, size) in enumerate(sums):
+        for i, (t, s, size) in enumerate(chunks):
             for l in LAYERS:
                 if s == 0:
                     load(p, l, t).wait()
@@ -163,30 +160,41 @@
     everything = jnp.sum(everything, axis=(0, 1), keepdims=True)
     factor = jnp.minimum(1.0, 0.5 * lax.rsqrt(everything / count + 1e-30))
 
-    rest = news[3]
+    def kind(q, last, i):
+        return 0 if q < last else 2 if i in left else 1
 
     def spread(q, l, i):
-        t, s, size = news[i]
+        t, s, size = chunks[i]
         block = (chip, chip, sides[l])[q]
         part = (l, at(block), pl.ds(s, size))
         to = (sides[1 - l], sides[l], sides[1 - l])[q]
-        return remote(new[t].at[part], new[t].at[part], ici_send.at[q // 2, t], ici_recv.at[q, l, i], at(to))
+        return remote(new[t].at[part], new[t].at[part], ici_send.at[kind(q, 2, i), t], ici_recv.at[q, l, i], at(to))
 
     def came(q, l):
         return (sides[l], sides[1 - l], far)[q]
 
     def share(q, l, i):
-        t, s, size = news[i]
+        t, s, size = chunks[i]
         block = chip if q == 0 else came(q - 1, l)
         part = (l, at(block), pl.ds(s, size))
         arrived = d2d_recv.at[3, l, i] if q == 3 else d2d_recv.at[0, 0, t]
-        return remote(new[t].at[part], new[t].at[part], d2d_send.at[q // 3, t], arrived, partner)
-
-    def keep(l):
-        t, s, size = rest
-        return pltpu.make_async_copy(new[t].at[l, at(sides[l]), pl.ds(s, size)], piece[l], piece_sem.at[l])
-
-    for i, (t, s, size) in enumerate(news):
+        return remote(new[t].at[part], new[t].at[part], d2d_send.at[kind(q, 3, i), t], arrived, partner)
+
+    def keep(l, i):
+        t, s, size = chunks[i]
+        first = sum(chunks[k][2] for k in left if k < i)
+
+        @pl.loop(0, size)
+        def _(r):
+            piece[first + r] = new[t][l, at(sides[l]), s + r]
+
+    def passes(l, i, action):
+        if i in left:
+            pl.when(core != l)(action)
+        else:
+            action()
+
+    for i, (t, s, size) in enumerate(chunks):
         for l in LAYERS:
 
             @pl.loop(s, s + size)
@@ -202,39 +210,46 @@
 
             spread(0, l, i).start()
             share(0, l, i).start()
-    for i in range(len(news)):
+    for i in range(len(chunks)):
         for l in LAYERS:
             spread(1, l, i).start()
     for k in range(1, n):
         told(k).wait_send()
     for q in range(3):
-        for i in range(len(news)):
+        for i in range(len(chunks)):
             for l in LAYERS:
-                if q == 2 and news[i] == rest:
-                    continue
-                spread(q, l, i).wait_recv()
-                if q == 0 and news[i] == rest:
-                    keep(l).start()
-                elif q == 0:
-                    spread(2, l, i).start()
-                share(q + 1, l, i).start()
+
+                def arrival(q=q, l=l, i=i):
+                    spread(q, l, i).wait_recv()
+                    share(q + 1, l, i).start()
+
+                if q < 2:
+                    spread(q, l, i).wait_recv()
+                    if q == 0:
+                        passes(l, i, lambda l=l, i=i: spread(2, l, i).start())
+                    share(q + 1, l, i).start()
+                    if q == 0 and i in left:
+                        pl.when(core == l)(lambda l=l, i=i: keep(l, i))
+                else:
+                    passes(l, i, arrival)
         if q == 1:
-            for l in LAYERS:
-                keep(l).wait()
             for t in range(3):
                 sent(t, 2, ici_send.at[0, t])
     for t in range(3):
         sent(t, 3, d2d_recv.at[0, 0, t])
         sent(t, 3, d2d_send.at[0, t])
-    for i in range(len(news)):
+    for i in range(len(chunks)):
         for l in LAYERS:
-            if news[i] != rest:
+            if i in left:
+                pl.when(core == l)(lambda l=l, i=i: share(3, l, i).wait_recv())
+            else:
                 share(3, l, i).wait_recv()
     for t in range(3):
-        units = rest[1] if t == rest[0] else new[t].shape[2]
-        part = new[t].at[:, pl.ds(0, 1), pl.ds(0, units)]
-        pltpu.make_async_copy(part, part, d2d_send.at[1, t]).wait()
-        pltpu.make_async_copy(part, part, ici_send.at[1, t]).wait()
+        units = sum(chunks[i][2] for i in left if chunks[i][0] == t)
+        for part, sems in ((new[t].at[:, 0, pl.ds(0, new[t].shape[2] - units)], 1), (new[t].at[0, 0, pl.ds(0, units)], 2)):
+            if part.shape[-3]:
+                pltpu.make_async_copy(part, part, d2d_send.at[sems, t]).wait()
+                pltpu.make_async_copy(part, part, ici_send.at[sems, t]).wait()
 
 
 def put_out(k, *refs):
@@ -260,15 +275,16 @@
     )(*arrays)
 
 
-def patch(n, down, *refs):
-    parts, out, sem = refs[:4], refs[4], refs[5]
+def patch(n, places, *refs):
+    parts, outs, sem = refs[2:4], refs[4:6], refs[6]
     me = lax.axis_index("dp")
     far, core = (me // 2 + 2) % (n // 2), me % 2
-    first = out.shape[2] - parts[0].shape[0]
     copies = []
-    for i, part in enumerate(parts):
-        block = far * 2 + (core if i < 2 else 1 - core)
-        copies.append(pltpu.make_async_copy(part, out.at[i % 2, block, pl.ds(first, part.shape[0])], sem.at[i]))
+    for i, of in enumerate((core, 1 - core)):
+        first = 0
+        for k, (t, s, size) in enumerate(places):
+            copies.append(pltpu.make_async_copy(parts[i].at[pl.ds(first, size)], outs[t].at[of, far * 2 + of, pl.ds(s, size)], sem.at[i, k]))
+            first += size
     for copy in copies:
         copy.start()
     for copy in copies:
@@ -281,8 +297,7 @@
 def solution(mesh):
     n = mesh.shape["dp"]
     chips = n // 2
-    ring = [(2 * c + k, 2 * ((c + 1) % chips) + k) for c in range(chips) for k in range(2)]
-    back = [(b, a) for a, b in ring]
+    ring = [(2 * c + k, 2 * ((c + (1, chips - 1)[k]) % chips) + k) for c in range(chips) for k in range(2)]
     swap = [(d, d + 1 - 2 * (d % 2)) for d in range(n)]
 
     def step(*arrays):
@@ -290,48 +305,45 @@
         layers = weights[0].shape[0]
         units = [one.shape[1] // ROWS for one in ms]
         cols = [one.shape[2] for one in ms]
-        sums, news = chunks_of(units)
+        chunks, left = chunks_of(units)
         count = n * sum(one.size for one in ms)
         whole = [(layers, n, u, ROWS, c) for u, c in zip(units, cols)]
         part = [(layers, u, ROWS, c) for u, c in zip(units, cols)]
-        left = (news[3][2], ROWS, cols[2])
+        over = (sum(chunks[i][2] for i in left), ROWS, cols[0])
         operands = (
             [t.reshape(s) for t, s in zip(terms, whole)]
             + [x.reshape(s) for x, s in zip(weights, whole)]
             + [x.reshape(s) for x, s in zip(ms, part)]
             + [x.reshape(s) for x, s in zip(vs, part)]
         )
-        k = max(len(sums), len(news))
+        k = len(chunks)
         dma = pltpu.SemaphoreType.DMA
         outs = pl.pallas_call(
-            functools.partial(kernel, n, count, sums, news),
+            functools.partial(kernel, n, count, chunks, left),
             name="step",
-            out_shape=[pltpu.VMEM(s, BF16) for s in whole] + [pltpu.VMEM(s, F32) for s in part] * 2 + [pltpu.HBM(left, BF16)] * 2,
+            out_shape=[pltpu.VMEM(s, BF16) for s in whole] + [pltpu.VMEM(s, F32) for s in part] * 2 + [pltpu.VMEM(over, BF16)],
             in_specs=[IN_HBM] * 12,
-            out_specs=[IN_VMEM] * 9 + [IN_HBM] * 2,
+            out_specs=[IN_VMEM] * 10,
             scratch_shapes=[pltpu.VMEM((2, *s[1:]), BF16) for s in part]
             + [pltpu.VMEM(s, BF16) for s in part]
             + [pltpu.VMEM((ROWS, 128), F32), pltpu.VMEM((n, 1, 128), F32)]
-            + [dma((2, 3)), dma((4, 2, k)), dma((2, 3)), dma((3, 2, k)), dma((2, 3)), dma((3, 3)), dma((n,)), dma((n,)), dma((2,))],
+            + [dma((3, 3)), dma((4, 2, k)), dma((3, 3)), dma((3, 2, k)), dma((2, 3)), dma((3, 3)), dma((n,)), dma((n,))],
             compiler_params=pltpu.CompilerParams(collective_id=0, has_side_effects=True, vmem_limit_bytes=VMEM_LIMIT),
         )(*[pltpu.with_memory_space_constraint(o, pltpu.HBM) for o in operands])
-        gate, up, down, *moments = outs[:9]
-        over = [lax.ppermute(outs[9], "dp", ring), lax.ppermute(outs[10], "dp", back)]
-        first = written("put_first", *moments, gate, up)
-        over[0], over[1] = lax.optimization_barrier((*over, first[0]))[:2]
-        across = [lax.ppermute(o, "dp", swap) for o in over]
-        (last,) = written("put_last", down)
-        new_down = pl.pallas_call(
-            functools.partial(patch, n),
+        over = lax.ppermute(outs[9], "dp", ring)
+        outs = list(written("put_out", *outs[:9]))
+        over = lax.optimization_barrier((over, outs[8]))[0]
+        across = lax.ppermute(over, "dp", swap)
+        outs[:2] = pl.pallas_call(
+            functools.partial(patch, n, [chunks[i] for i in left]),
             name="patch",
-            out_shape=pltpu.HBM(last.shape, BF16),
-            in_specs=[IN_HBM] + [IN_VMEM] * 4,
-            out_specs=IN_HBM,
-            scratch_shapes=[dma((4,))],
-            input_output_aliases={0: 0},
+            out_shape=[pltpu.HBM(o.shape, BF16) for o in outs[:2]],
+            in_specs=[IN_HBM] * 2 + [IN_VMEM] * 2,
+            out_specs=[IN_HBM] * 2,
+            scratch_shapes=[dma((2, len(left)))],
+            input_output_aliases={0: 0, 1: 1},
             compiler_params=pltpu.CompilerParams(has_side_effects=True, vmem_limit_bytes=VMEM_LIMIT),
-        )(last, *[pltpu.with_memory_space_constraint(o, pltpu.VMEM) for o in over + across])
-        outs = (first[6], first[7], new_down, *first[:6])
+        )(*outs[:2], *[pltpu.with_memory_space_constraint(o, pltpu.VMEM) for o in (over, across)])
         shapes = [x.shape for x in weights] + [x.shape for x in ms] * 2
         return tuple(o.reshape(s) for o, s in zip(outs, shapes))
 

time: 248 us -> 247 us (level)
  Pallas kernels: 244 us -> 241 us
    pallas_call x2 -> x1, Pallas kernels: 14.4 us -> 13.4 us  [written(): pl.pallas_call(functools.partial(put_out, k), name=name, out_shape=[pltpu...]
  transfers between devices with their start and end apart: 4 -> 2, of which waited for: 0 -> 1; matrix products, arithmetic and copies ran while one was open for 0% -> 0% of each run, Pallas kernels for 6% -> 5%
where the time goes in v3:
time: 247 us
  Pallas kernels  241 us (98%)
  starting transfers between devices  3.16 us (1%)
    pallas_call x1, Pallas kernels, step(): pl.pallas_call(functools.partial(kernel, n, count, chunks, left), name='s...  226 us
    pallas_call x1, Pallas kernels, written(): pl.pallas_call(functools.partial(put_out, k), name=name, out_shape=[pltpu...  13.4 us
  transfers between devices with their start and end apart: 2, of which 1 were waited for; matrix products, arithmetic and copies ran while one was open for 0% of the time, Pallas kernels for 5%

profile of v3, /device:TPU:113, one launch (start us, length us, event | category | flops | bytes accessed | tf_op | source)
XLA Modules:
  0.0 246.8 jit_solution(5262816575191742546)
XLA Ops:
  0.6 225.9 %step.1 = (bf16[2,8,7,16,2560]{4,3,2,1,0:T(8,128)(2,1)S(1)}, bf16[2,8,7,16,2560]{4,3,2,1,0:T(8,128)(2,1)S(1)}, bf16[2,8,20,16,896]{4,3,2,1,0:T(8,128)(2,1)S(1)},...) custom-call(bf16[2,8,7,16,2560]{4,3,2,1,0:T(8,128)(2,1)} %bitcast.23, ...), custom_call_target="tpu_custom_call" | custom-call | tf_op jit(solution)/shard_map/step/pallas_call | solution.py:321
  226.5 2.1 collective-permute-start
  228.6 13.4 %put_out.1 = (bf16[2,8,7,16,2560]{4,3,2,1,0:T(8,128)(2,1)}, bf16[2,8,7,16,2560]{4,3,2,1,0:T(8,128)(2,1)}, bf16[2,8,20,16,896]{4,3,2,1,0:T(8,128)(2,1)}, f32[2,7,...) custom-call(bf16[2,8,7,16,2560]{4,3,2,1,0:T(8,128)(2,1)S(1)} %get-tu, ...), custom_call_target="tpu_custom_call" | custom-call | flops 4128768000 | bytes 41287680 | tf_op jit(solution)/shard_map/put_out/pallas_call | solution.py:266
  242.1 0.0 collective-permute-done.refs_2_
  242.1 1.1 collective-permute-start.1
  243.1 2.3 collective-permute-done.1.refs_3_
  245.5 1.4 patch.1
Async XLA Ops:
  226.5 15.5 %collective-permute-start = (bf16[13,16,2560]{2,1,0:T(8,128)(2,1)S(1)}, bf16[13,16,2560]{2,1,0:T(8,128)(2,1)S(1)}, u32[]{:S(2)}, u32[]{:S(2)}) collective-permute-start(bf16[13,16,2560]{2,1,0:T(8,128)(2,1)S(1)} %get-tuple-element.42), channel_id=1, source_target_pairs={{0,2},{1,7},{2,4},{3,1},{4,6},{5,3},{6,0},{7,5},{8,10},{9,15},{10,... | collective-permute-start | bytes 3194888 | tf_op jit(solution)/shard_map/ppermute | solution.py:333
  242.1 3.4 %collective-permute-start.1 = (bf16[13,16,2560]{2,1,0:T(8,128)(2,1)S(1)}, bf16[13,16,2560]{2,1,0:T(8,128)(2,1)S(1)}, u32[]{:S(2)}, u32[]{:S(2)}) collective-permute-start(bf16[13,16,2560]{2,1,0:T(8,128)(2,1)S(1)} %collective-permute-done.refs_2_), channel_id=1, source_target_pairs={{0,1},{1,0},{2,3},{3,2},{4,5},{5,4},{6,7},{7,6},{8,9},{9,8},{10,11... | collective-permute-start | bytes 3194888 | tf_op jit(solution)/shard_map/ppermute | solution.py:336

commit v4 on v3

--- a/solution.py
+++ b/solution.py
@@ -17,12 +17,14 @@
 def chunks_of(units):
     gate, up, down = units
     a, b = gate // 7, 3 * gate // 7
-    c, d, e = 12 * down // 20, 17 * down // 20, 19 * down // 20
-    chunks = [(0, 0, a), (0, a, b - a), (0, b, gate - b), (1, 0, up), (2, 0, c), (2, c, d - c), (2, d, e - d), (2, e, down - e)]
-    return chunks, (1, 2, 3)
-
-
-def kernel(n, count, chunks, left, *refs):
+    head = [(0, 0, a), (0, a, b - a), (0, b, gate - b), (1, 0, up)]
+    c = down - down // 10
+    sums = head + [(2, 0, c), (2, c, down - c)]
+    cuts = [k * down // 20 for k in (0, 14, 18, 20)]
+    return sums, head + [(2, c, d - c) for c, d in zip(cuts, cuts[1:])], (1, 2, 3)
+
+
+def kernel(n, count, sums, chunks, left, *refs):
     g, w, m_in, v_in = refs[0:3], refs[3:6], refs[6:9], refs[9:12]
     new, m, v = refs[12:15], refs[15:18], refs[18:21]
     piece = refs[21]
@@ -65,18 +67,18 @@
             load(0, l, t).start()
 
     barrier = pltpu.get_barrier_semaphore()
-    for k in range(1, n):
-        pl.semaphore_signal(barrier, inc=1, device_id={"dp": (me + k) % n}, device_id_type=MESH)
-    pl.semaphore_wait(barrier, n - 1)
+    for k in (partner, at(down_), at(up_)):
+        pl.semaphore_signal(barrier, inc=1, device_id={"dp": k}, device_id_type=MESH)
+    pl.semaphore_wait(barrier, 3)
 
     def handed(p, l, i):
-        t, s, size = chunks[i]
+        t, s, size = sums[i]
         there = blocks[p][l] * 2 + 1 - core
         part = (l, there, pl.ds(s, size))
         return remote(g[t].at[part], new[t].at[part], d2d_send.at[0, t], d2d_recv.at[p, l, i], partner)
 
     for p in range(4):
-        for i in range(len(chunks)):
+        for i in range(len(sums)):
             for l in LAYERS:
                 handed(p, l, i).start()
 
@@ -84,7 +86,7 @@
         return j * 2 + 1 - core
 
     def passed(p, l, i):
-        t, s, size = chunks[i]
+        t, s, size = sums[i]
         return remote(
             new[t].at[l, at(blocks[p][l]), pl.ds(s, size)],
             new[t].at[l, inbox(p), pl.ds(s, size)],
@@ -96,7 +98,7 @@
     total[...] = jnp.zeros_like(total)
 
     def add(p, l, i):
-        t, s, size = chunks[i]
+        t, s, size = sums[i]
         block = at(blocks[p][l])
 
         @pl.loop(s, s + size)
@@ -117,7 +119,7 @@
                 total[...] += parts[0]
 
     for p in range(4):
-        for i, (t, s, size) in enumerate(chunks):
+        for i, (t, s, size) in enumerate(sums):
             for l in LAYERS:
                 if s == 0:
                     load(p, l, t).wait()
@@ -275,20 +277,33 @@
     )(*arrays)
 
 
-def patch(n, places, *refs):
-    parts, outs, sem = refs[2:4], refs[4:6], refs[6]
+def patch(n, own, places, *refs):
+    piece, outs, sem = refs[2], refs[3:5], refs[5]
     me = lax.axis_index("dp")
     far, core = (me // 2 + 2) % (n // 2), me % 2
-    copies = []
-    for i, of in enumerate((core, 1 - core)):
-        first = 0
-        for k, (t, s, size) in enumerate(places):
-            copies.append(pltpu.make_async_copy(parts[i].at[pl.ds(first, size)], outs[t].at[of, far * 2 + of, pl.ds(s, size)], sem.at[i, k]))
-            first += size
+    of = core if own else 1 - core
+    copies, first = [], 0
+    for k, (t, s, size) in enumerate(places):
+        copies.append(pltpu.make_async_copy(piece.at[pl.ds(first, size)], outs[t].at[of, far * 2 + of, pl.ds(s, size)], sem.at[k]))
+        first += size
     for copy in copies:
         copy.start()
     for copy in copies:
         copy.wait()
+
+
+def patched(name, n, own, places, outs, piece):
+    return pl.pallas_call(
+        functools.partial(patch, n, own, places),
+        name=name,
+        out_shape=[pltpu.HBM(o.shape, BF16) for o in outs],
+        in_specs=[IN_HBM] * 2 + [IN_VMEM],
+        out_specs=[IN_HBM] * 2,
+        scratch_shapes=[pltpu.SemaphoreType.DMA((len(places),))],
+        input_output_aliases={0: 0, 1: 1},
+        cost_estimate=pl.CostEstimate(flops=100 * piece.size, bytes_accessed=2 * piece.size, transcendentals=0),
+        compiler_params=pltpu.CompilerParams(has_side_effects=True, vmem_limit_bytes=VMEM_LIMIT),
+    )(*outs, pltpu.with_memory_space_constraint(piece, pltpu.VMEM))
 
 
 IN_VMEM, IN_HBM = pl.BlockSpec(memory_space=pltpu.VMEM), pl.BlockSpec(memory_space=pltpu.HBM)
@@ -305,7 +320,7 @@
         layers = weights[0].shape[0]
         units = [one.shape[1] // ROWS for one in ms]
         cols = [one.shape[2] for one in ms]
-        chunks, left = chunks_of(units)
+        sums, chunks, left = chunks_of(units)
         count = n * sum(one.size for one in ms)
         whole = [(layers, n, u, ROWS, c) for u, c in zip(units, cols)]
         part = [(layers, u, ROWS, c) for u, c in zip(units, cols)]
@@ -316,10 +331,10 @@
             + [x.reshape(s) for x, s in zip(ms, part)]
             + [x.reshape(s) for x, s in zip(vs, part)]
         )
-        k = len(chunks)
+        k = max(len(sums), len(chunks))
         dma = pltpu.SemaphoreType.DMA
         outs = pl.pallas_call(
-            functools.partial(kernel, n, count, chunks, left),
+            functools.partial(kernel, n, count, sums, chunks, left),
             name="step",
             out_shape=[pltpu.VMEM(s, BF16) for s in whole] + [pltpu.VMEM(s, F32) for s in part] * 2 + [pltpu.VMEM(over, BF16)],
             in_specs=[IN_HBM] * 12,
@@ -334,16 +349,9 @@
         outs = list(written("put_out", *outs[:9]))
         over = lax.optimization_barrier((over, outs[8]))[0]
         across = lax.ppermute(over, "dp", swap)
-        outs[:2] = pl.pallas_call(
-            functools.partial(patch, n, [chunks[i] for i in left]),
-            name="patch",
-            out_shape=[pltpu.HBM(o.shape, BF16) for o in outs[:2]],
-            in_specs=[IN_HBM] * 2 + [IN_VMEM] * 2,
-            out_specs=[IN_HBM] * 2,
-            scratch_shapes=[dma((2, len(left)))],
-            input_output_aliases={0: 0, 1: 1},
-            compiler_params=pltpu.CompilerParams(has_side_effects=True, vmem_limit_bytes=VMEM_LIMIT),
-        )(*outs[:2], *[pltpu.with_memory_space_constraint(o, pltpu.VMEM) for o in (over, across)])
+        places = [chunks[i] for i in left]
+        outs[:2] = patched("patch_own", n, True, places, outs[:2], over)
+        outs[:2] = patched("patch_partner", n, False, places, outs[:2], across)
         shapes = [x.shape for x in weights] + [x.shape for x in ms] * 2
         return tuple(o.reshape(s) for o, s in zip(outs, shapes))
 

time: 247 us -> 246 us (level)
    pallas_call x2 -> x3, Pallas kernels: 227 us -> 227 us  [the longest x1 225 us: step(): pl.pallas_call(functools.partial(kernel, n, count, sums, chunks, left), n...]
  transfers between devices with their start and end apart: 2 -> 2, of which waited for: 1 -> 1; matrix products, arithmetic and copies ran while one was open for 0% -> 0% of each run, Pallas kernels for 5% -> 6%
where the time goes in v4:
time: 246 us
  Pallas kernels  241 us (98%)
  starting transfers between devices  3.07 us (1%)
    pallas_call x1, Pallas kernels, step(): pl.pallas_call(functools.partial(kernel, n, count, sums, chunks, left), n...  225 us
    pallas_call x1, Pallas kernels, written(): pl.pallas_call(functools.partial(put_out, k), name=name, out_shape=[pltpu...  13.4 us
  transfers between devices with their start and end apart: 2, of which 1 were waited for; matrix products, arithmetic and copies ran while one was open for 0% of the time, Pallas kernels for 6%

profile of v4, /device:TPU:113, one launch (start us, length us, event | category | flops | bytes accessed | tf_op | source)
XLA Modules:
  0.0 245.9 jit_solution(2795014000459784852)
XLA Ops:
  0.6 225.4 %step.1 = (bf16[2,8,7,16,2560]{4,3,2,1,0:T(8,128)(2,1)S(1)}, bf16[2,8,7,16,2560]{4,3,2,1,0:T(8,128)(2,1)S(1)}, bf16[2,8,20,16,896]{4,3,2,1,0:T(8,128)(2,1)S(1)},...) custom-call(bf16[2,8,7,16,2560]{4,3,2,1,0:T(8,128)(2,1)} %bitcast.23, ...), custom_call_target="tpu_custom_call" | custom-call | tf_op jit(solution)/shard_map/step/pallas_call | solution.py:336
  226.1 2.1 collective-permute-start
  228.2 13.4 %put_out.1 = (bf16[2,8,7,16,2560]{4,3,2,1,0:T(8,128)(2,1)}, bf16[2,8,7,16,2560]{4,3,2,1,0:T(8,128)(2,1)}, bf16[2,8,20,16,896]{4,3,2,1,0:T(8,128)(2,1)}, f32[2,7,...) custom-call(bf16[2,8,7,16,2560]{4,3,2,1,0:T(8,128)(2,1)S(1)} %get-tu, ...), custom_call_target="tpu_custom_call" | custom-call | flops 4128768000 | bytes 41287680 | tf_op jit(solution)/shard_map/put_out/pallas_call | solution.py:268
  241.7 0.0 collective-permute-done.refs_2_
  241.7 0.9 collective-permute-start.1
  242.6 1.0 patch_own.1
  243.6 1.3 collective-permute-done.1.refs_2_
  244.9 1.0 patch_partner.1
Async XLA Ops:
  226.1 15.6 %collective-permute-start = (bf16[13,16,2560]{2,1,0:T(8,128)(2,1)S(1)}, bf16[13,16,2560]{2,1,0:T(8,128)(2,1)S(1)}, u32[]{:S(2)}, u32[]{:S(2)}) collective-permute-start(bf16[13,16,2560]{2,1,0:T(8,128)(2,1)S(1)} %get-tuple-element.44), channel_id=1, source_target_pairs={{0,2},{1,7},{2,4},{3,1},{4,6},{5,3},{6,0},{7,5},{8,10},{9,15},{10,... | collective-permute-start | bytes 3194888 | tf_op jit(solution)/shard_map/ppermute | solution.py:348
  241.7 3.2 %collective-permute-start.1 = (bf16[13,16,2560]{2,1,0:T(8,128)(2,1)S(1)}, bf16[13,16,2560]{2,1,0:T(8,128)(2,1)S(1)}, u32[]{:S(2)}, u32[]{:S(2)}) collective-permute-start(bf16[13,16,2560]{2,1,0:T(8,128)(2,1)S(1)} %collective-permute-done.refs_2_), channel_id=1, source_target_pairs={{0,1},{1,0},{2,3},{3,2},{4,5},{5,4},{6,7},{7,6},{8,9},{9,8},{10,11... | collective-permute-start | bytes 3194888 | tf_op jit(solution)/shard_map/ppermute | solution.py:351

commit v5 on v4

--- a/solution.py
+++ b/solution.py
@@ -17,11 +17,11 @@
 def chunks_of(units):
     gate, up, down = units
     a, b = gate // 7, 3 * gate // 7
-    head = [(0, 0, a), (0, a, b - a), (0, b, gate - b), (1, 0, up)]
+    head = [(0, 0, a), (0, a, gate - a), (1, 0, up)]
     c = down - down // 10
     sums = head + [(2, 0, c), (2, c, down - c)]
     cuts = [k * down // 20 for k in (0, 14, 18, 20)]
-    return sums, head + [(2, c, d - c) for c, d in zip(cuts, cuts[1:])], (1, 2, 3)
+    return sums, head + [(2, c, d - c) for c, d in zip(cuts, cuts[1:])], (1, 2)
 
 
 def kernel(n, count, sums, chunks, left, *refs):

time: 246 us -> 246 us (level)
  no operation moved by 1% of the time
where the time goes in v5:
time: 246 us
  Pallas kernels  241 us (98%)
  starting transfers between devices  3.17 us (1%)
    pallas_call x1, Pallas kernels, step(): pl.pallas_call(functools.partial(kernel, n, count, sums, chunks, left), n...  225 us
    pallas_call x1, Pallas kernels, written(): pl.pallas_call(functools.partial(put_out, k), name=name, out_shape=[pltpu...  13.4 us
  transfers between devices with their start and end apart: 2, of which 1 were waited for; matrix products, arithmetic and copies ran while one was open for 0% of the time, Pallas kernels for 6%

profile of v5, /device:TPU:113, one launch (start us, length us, event | category | flops | bytes accessed | tf_op | source)
XLA Modules:
  0.0 245.7 jit_solution(13238847515181630408)
XLA Ops:
  0.6 225.2 %step.1 = (bf16[2,8,7,16,2560]{4,3,2,1,0:T(8,128)(2,1)S(1)}, bf16[2,8,7,16,2560]{4,3,2,1,0:T(8,128)(2,1)S(1)}, bf16[2,8,20,16,896]{4,3,2,1,0:T(8,128)(2,1)S(1)},...) custom-call(bf16[2,8,7,16,2560]{4,3,2,1,0:T(8,128)(2,1)} %bitcast.23, ...), custom_call_target="tpu_custom_call" | custom-call | tf_op jit(solution)/shard_map/step/pallas_call | solution.py:336
  225.8 2.1 collective-permute-start
  227.9 13.4 %put_out.1 = (bf16[2,8,7,16,2560]{4,3,2,1,0:T(8,128)(2,1)}, bf16[2,8,7,16,2560]{4,3,2,1,0:T(8,128)(2,1)}, bf16[2,8,20,16,896]{4,3,2,1,0:T(8,128)(2,1)}, f32[2,7,...) custom-call(bf16[2,8,7,16,2560]{4,3,2,1,0:T(8,128)(2,1)S(1)} %get-tu, ...), custom_call_target="tpu_custom_call" | custom-call | flops 4128768000 | bytes 41287680 | tf_op jit(solution)/shard_map/put_out/pallas_call | solution.py:268
  241.4 0.0 collective-permute-done.refs_2_
  241.4 1.1 collective-permute-start.1
  242.4 1.0 patch_own.1
  243.4 1.3 collective-permute-done.1.refs_2_
  244.8 1.0 patch_partner.1
Async XLA Ops:
  225.8 15.5 %collective-permute-start = (bf16[13,16,2560]{2,1,0:T(8,128)(2,1)S(1)}, bf16[13,16,2560]{2,1,0:T(8,128)(2,1)S(1)}, u32[]{:S(2)}, u32[]{:S(2)}) collective-permute-start(bf16[13,16,2560]{2,1,0:T(8,128)(2,1)S(1)} %get-tuple-element.44), channel_id=1, source_target_pairs={{0,2},{1,7},{2,4},{3,1},{4,6},{5,3},{6,0},{7,5},{8,10},{9,15},{10,... | collective-permute-start | bytes 3194888 | tf_op jit(solution)/shard_map/ppermute | solution.py:348
  241.4 3.4 %collective-permute-start.1 = (bf16[13,16,2560]{2,1,0:T(8,128)(2,1)S(1)}, bf16[13,16,2560]{2,1,0:T(8,128)(2,1)S(1)}, u32[]{:S(2)}, u32[]{:S(2)}) collective-permute-start(bf16[13,16,2560]{2,1,0:T(8,128)(2,1)S(1)} %collective-permute-done.refs_2_), channel_id=1, source_target_pairs={{0,1},{1,0},{2,3},{3,2},{4,5},{5,4},{6,7},{7,6},{8,9},{9,8},{10,11... | collective-permute-start | bytes 3194888 | tf_op jit(solution)/shard_map/ppermute | solution.py:351

commit v6 on v5

--- a/solution.py
+++ b/solution.py
@@ -192,7 +192,7 @@
 
     def passes(l, i, action):
         if i in left:
-            pl.when(core != l)(action)
+            pl.when(core == l)(action)
         else:
             action()
 
@@ -231,7 +231,7 @@
                         passes(l, i, lambda l=l, i=i: spread(2, l, i).start())
                     share(q + 1, l, i).start()
                     if q == 0 and i in left:
-                        pl.when(core == l)(lambda l=l, i=i: keep(l, i))
+                        pl.when(core != l)(lambda l=l, i=i: keep(l, i))
                 else:
                     passes(l, i, arrival)
         if q == 1:
@@ -243,7 +243,7 @@
     for i in range(len(chunks)):
         for l in LAYERS:
             if i in left:
-                pl.when(core == l)(lambda l=l, i=i: share(3, l, i).wait_recv())
+                pl.when(core != l)(lambda l=l, i=i: share(3, l, i).wait_recv())
             else:
                 share(3, l, i).wait_recv()
     for t in range(3):
@@ -284,7 +284,7 @@
     of = core if own else 1 - core
     copies, first = [], 0
     for k, (t, s, size) in enumerate(places):
-        copies.append(pltpu.make_async_copy(piece.at[pl.ds(first, size)], outs[t].at[of, far * 2 + of, pl.ds(s, size)], sem.at[k]))
+        copies.append(pltpu.make_async_copy(piece.at[pl.ds(first, size)], outs[t].at[1 - of, far * 2 + of, pl.ds(s, size)], sem.at[k]))
         first += size
     for copy in copies:
         copy.start()
@@ -312,7 +312,7 @@
 def solution(mesh):
     n = mesh.shape["dp"]
     chips = n // 2
-    ring = [(2 * c + k, 2 * ((c + (1, chips - 1)[k]) % chips) + k) for c in range(chips) for k in range(2)]
+    ring = [(2 * c + k, 2 * ((c + (chips - 1, 1)[k]) % chips) + k) for c in range(chips) for k in range(2)]
     swap = [(d, d + 1 - 2 * (d % 2)) for d in range(n)]
 
     def step(*arrays):

time: 246 us -> 245 us (level)
  starting transfers between devices: 3.17 us -> 0.35 us
  transfers between devices with their start and end apart: 2 -> 2, of which waited for: 1 -> 2; matrix products, arithmetic and copies ran while one was open for 0% -> 0% of each run, Pallas kernels for 6% -> 6%
where the time goes in v6:
time: 245 us
  Pallas kernels  241 us (98%)
  waiting for transfers between devices  3 us (1%)
    pallas_call x1, Pallas kernels, step(): pl.pallas_call(functools.partial(kernel, n, count, sums, chunks, left), n...  226 us
    pallas_call x1, Pallas kernels, written(): pl.pallas_call(functools.partial(put_out, k), name=name, out_shape=[pltpu...  13.4 us
  transfers between devices with their start and end apart: 2, of which 2 were waited for; matrix products, arithmetic and copies ran while one was open for 0% of the time, Pallas kernels for 6%

profile of v6, /device:TPU:113, one launch (start us, length us, event | category | flops | bytes accessed | tf_op | source)
XLA Modules:
  0.0 245.1 jit_solution(6676340893023316377)
XLA Ops:
  0.6 225.7 %step.1 = (bf16[2,8,7,16,2560]{4,3,2,1,0:T(8,128)(2,1)S(1)}, bf16[2,8,7,16,2560]{4,3,2,1,0:T(8,128)(2,1)S(1)}, bf16[2,8,20,16,896]{4,3,2,1,0:T(8,128)(2,1)S(1)},...) custom-call(bf16[2,8,7,16,2560]{4,3,2,1,0:T(8,128)(2,1)} %bitcast.23, ...), custom_call_target="tpu_custom_call" | custom-call | tf_op jit(solution)/shard_map/step/pallas_call | solution.py:336
  226.4 0.3 collective-permute-start
  226.6 13.4 %put_out.1 = (bf16[2,8,7,16,2560]{4,3,2,1,0:T(8,128)(2,1)}, bf16[2,8,7,16,2560]{4,3,2,1,0:T(8,128)(2,1)}, bf16[2,8,20,16,896]{4,3,2,1,0:T(8,128)(2,1)}, f32[2,7,...) custom-call(bf16[2,8,7,16,2560]{4,3,2,1,0:T(8,128)(2,1)S(1)} %get-tu, ...), custom_call_target="tpu_custom_call" | custom-call | flops 4128768000 | bytes 41287680 | tf_op jit(solution)/shard_map/put_out/pallas_call | solution.py:268
  240.1 1.4 collective-permute-done.refs_2_
  241.5 0.1 collective-permute-start.1
  241.6 1.0 patch_own.1
  242.6 1.6 collective-permute-done.1.refs_2_
  244.2 1.0 patch_partner.1
Async XLA Ops:
  226.4 15.1 %collective-permute-start = (bf16[13,16,2560]{2,1,0:T(8,128)(2,1)S(1)}, bf16[13,16,2560]{2,1,0:T(8,128)(2,1)S(1)}, u32[]{:S(2)}, u32[]{:S(2)}) collective-permute-start(bf16[13,16,2560]{2,1,0:T(8,128)(2,1)S(1)} %get-tuple-element.44), channel_id=1, source_target_pairs={{0,6},{1,3},{2,0},{3,5},{4,2},{5,7},{6,4},{7,1},{8,14},{9,11},{10,... | collective-permute-start | bytes 3194888 | tf_op jit(solution)/shard_map/ppermute | solution.py:348
  241.5 2.7 %collective-permute-start.1 = (bf16[13,16,2560]{2,1,0:T(8,128)(2,1)S(1)}, bf16[13,16,2560]{2,1,0:T(8,128)(2,1)S(1)}, u32[]{:S(2)}, u32[]{:S(2)}) collective-permute-start(bf16[13,16,2560]{2,1,0:T(8,128)(2,1)S(1)} %collective-permute-done.refs_2_), channel_id=1, source_target_pairs={{0,1},{1,0},{2,3},{3,2},{4,5},{5,4},{6,7},{7,6},{8,9},{9,8},{10,11... | collective-permute-start | bytes 3194888 | tf_op jit(solution)/shard_map/ppermute | solution.py:351

commit v7 on v6

--- a/solution.py
+++ b/solution.py
@@ -20,7 +20,7 @@
     head = [(0, 0, a), (0, a, gate - a), (1, 0, up)]
     c = down - down // 10
     sums = head + [(2, 0, c), (2, c, down - c)]
-    cuts = [k * down // 20 for k in (0, 14, 18, 20)]
+    cuts = [k * down // 20 for k in (0, 15, 19, 20)]
     return sums, head + [(2, c, d - c) for c, d in zip(cuts, cuts[1:])], (1, 2)
 
 
@@ -150,7 +150,7 @@
         return remote(squares.at[me], squares.at[me], sq_send.at[k], sq_recv.at[k], (me + k) % n)
 
     squares[me] = jnp.sum(total[...], axis=0, keepdims=True)
-    for k in range(1, n):
+    for k in sorted(range(1, n), key=lambda k: -min(k, n - k)):
         told(k).start()
     for copy in state():
         copy.wait()

time: 245 us -> 245 us (level)
  no operation moved by 1% of the time
where the time goes in v7:
time: 245 us
  Pallas kernels  241 us (98%)
  waiting for transfers between devices  2.93 us (1%)
    pallas_call x1, Pallas kernels, step(): pl.pallas_call(functools.partial(kernel, n, count, sums, chunks, left), n...  226 us
    pallas_call x1, Pallas kernels, written(): pl.pallas_call(functools.partial(put_out, k), name=name, out_shape=[pltpu...  13.4 us
  transfers between devices with their start and end apart: 2, of which 2 were waited for; matrix products, arithmetic and copies ran while one was open for 0% of the time, Pallas kernels for 6%

profile of v7, /device:TPU:113, one launch (start us, length us, event | category | flops | bytes accessed | tf_op | source)
XLA Modules:
  0.0 245.1 jit_solution(7444323471677419388)
XLA Ops:
  0.6 225.6 %step.1 = (bf16[2,8,7,16,2560]{4,3,2,1,0:T(8,128)(2,1)S(1)}, bf16[2,8,7,16,2560]{4,3,2,1,0:T(8,128)(2,1)S(1)}, bf16[2,8,20,16,896]{4,3,2,1,0:T(8,128)(2,1)S(1)},...) custom-call(bf16[2,8,7,16,2560]{4,3,2,1,0:T(8,128)(2,1)} %bitcast.23, ...), custom_call_target="tpu_custom_call" | custom-call | tf_op jit(solution)/shard_map/step/pallas_call | solution.py:336
  226.3 0.3 collective-permute-start
  226.6 13.4 %put_out.1 = (bf16[2,8,7,16,2560]{4,3,2,1,0:T(8,128)(2,1)}, bf16[2,8,7,16,2560]{4,3,2,1,0:T(8,128)(2,1)}, bf16[2,8,20,16,896]{4,3,2,1,0:T(8,128)(2,1)}, f32[2,7,...) custom-call(bf16[2,8,7,16,2560]{4,3,2,1,0:T(8,128)(2,1)S(1)} %get-tu, ...), custom_call_target="tpu_custom_call" | custom-call | flops 4128768000 | bytes 41287680 | tf_op jit(solution)/shard_map/put_out/pallas_call | solution.py:268
  240.0 1.4 collective-permute-done.refs_2_
  241.4 0.1 collective-permute-start.1
  241.5 1.0 patch_own.1
  242.5 1.6 collective-permute-done.1.refs_2_
  244.1 1.0 patch_partner.1
Async XLA Ops:
  226.3 15.1 %collective-permute-start = (bf16[13,16,2560]{2,1,0:T(8,128)(2,1)S(1)}, bf16[13,16,2560]{2,1,0:T(8,128)(2,1)S(1)}, u32[]{:S(2)}, u32[]{:S(2)}) collective-permute-start(bf16[13,16,2560]{2,1,0:T(8,128)(2,1)S(1)} %get-tuple-element.44), channel_id=1, source_target_pairs={{0,6},{1,3},{2,0},{3,5},{4,2},{5,7},{6,4},{7,1},{8,14},{9,11},{10,... | collective-permute-start | bytes 3194888 | tf_op jit(solution)/shard_map/ppermute | solution.py:348
  241.4 2.7 %collective-permute-start.1 = (bf16[13,16,2560]{2,1,0:T(8,128)(2,1)S(1)}, bf16[13,16,2560]{2,1,0:T(8,128)(2,1)S(1)}, u32[]{:S(2)}, u32[]{:S(2)}) collective-permute-start(bf16[13,16,2560]{2,1,0:T(8,128)(2,1)S(1)} %collective-permute-done.refs_2_), channel_id=1, source_target_pairs={{0,1},{1,0},{2,3},{3,2},{4,5},{5,4},{6,7},{7,6},{8,9},{9,8},{10,11... | collective-permute-start | bytes 3194888 | tf_op jit(solution)/shard_map/ppermute | solution.py:351

commit v8 on v7

--- a/solution.py
+++ b/solution.py
@@ -21,7 +21,7 @@
     c = down - down // 10
     sums = head + [(2, 0, c), (2, c, down - c)]
     cuts = [k * down // 20 for k in (0, 15, 19, 20)]
-    return sums, head + [(2, c, d - c) for c, d in zip(cuts, cuts[1:])], (1, 2)
+    return sums, head + [(2, c, d - c) for c, d in zip(cuts, cuts[1:])], (0, 1, 2)
 
 
 def kernel(n, count, sums, chunks, left, *refs):
@@ -346,11 +346,13 @@
             compiler_params=pltpu.CompilerParams(collective_id=0, has_side_effects=True, vmem_limit_bytes=VMEM_LIMIT),
         )(*[pltpu.with_memory_space_constraint(o, pltpu.HBM) for o in operands])
         over = lax.ppermute(outs[9], "dp", ring)
-        outs = list(written("put_out", *outs[:9]))
-        over = lax.optimization_barrier((over, outs[8]))[0]
+        early, late = outs[: 9 - 1], outs[9 - 1 : 9]
+        outs = list(written("put_out", *early))
+        over = lax.optimization_barrier((over, outs[-1]))[0]
         across = lax.ppermute(over, "dp", swap)
         places = [chunks[i] for i in left]
         outs[:2] = patched("patch_own", n, True, places, outs[:2], over)
+        outs += written("put_late", *late)
         outs[:2] = patched("patch_partner", n, False, places, outs[:2], across)
         shapes = [x.shape for x in weights] + [x.shape for x in ms] * 2
         return tuple(o.reshape(s) for o, s in zip(outs, shapes))

time: 245 us -> 245 us (level)
    pallas_call x1 -> x2, Pallas kernels: 13.4 us -> 14.1 us  [written(): pl.pallas_call(functools.partial(put_out, k), name=name, out_shape=[pltpu...]
where the time goes in v8:
time: 245 us
  Pallas kernels  241 us (98%)
  waiting for transfers between devices  3.22 us (1%)
    pallas_call x1, Pallas kernels, step(): pl.pallas_call(functools.partial(kernel, n, count, sums, chunks, left), n...  225 us
    pallas_call x2, Pallas kernels, written(): pl.pallas_call(functools.partial(put_out, k), name=name, out_shape=[pltpu...  14.1 us
  transfers between devices with their start and end apart: 2, of which 2 were waited for; matrix products, arithmetic and copies ran while one was open for 0% of the time, Pallas kernels for 6%

profile of v8, /device:TPU:113, one launch (start us, length us, event | category | flops | bytes accessed | tf_op | source)
XLA Modules:
  0.0 245.2 jit_solution(11423910589633647907)
XLA Ops:
  0.6 224.7 %step.1 = (bf16[2,8,7,16,2560]{4,3,2,1,0:T(8,128)(2,1)S(1)}, bf16[2,8,7,16,2560]{4,3,2,1,0:T(8,128)(2,1)S(1)}, bf16[2,8,20,16,896]{4,3,2,1,0:T(8,128)(2,1)S(1)},...) custom-call(bf16[2,8,7,16,2560]{4,3,2,1,0:T(8,128)(2,1)} %bitcast.23, ...), custom_call_target="tpu_custom_call" | custom-call | tf_op jit(solution)/shard_map/step/pallas_call | solution.py:336
  225.4 0.3 collective-permute-start
  225.7 12.7 %put_out.1 = (bf16[2,8,7,16,2560]{4,3,2,1,0:T(8,128)(2,1)}, bf16[2,8,7,16,2560]{4,3,2,1,0:T(8,128)(2,1)}, bf16[2,8,20,16,896]{4,3,2,1,0:T(8,128)(2,1)}, f32[2,7,...) custom-call(bf16[2,8,7,16,2560]{4,3,2,1,0:T(8,128)(2,1)S(1)} %get-tu, ...), custom_call_target="tpu_custom_call" | custom-call | flops 3899392000 | bytes 38993920 | tf_op jit(solution)/shard_map/put_out/pallas_call | solution.py:268
  238.4 2.9 %collective-permute-done.refs_2_ = bf16[14,16,2560]{2,1,0:T(8,128)(2,1)S(1)} collective-permute-done((bf16[14,16,2560]{2,1,0:T(8,128)(2,1)S(1)}, bf16[14,16,2560]{2,1,0:T(8,128)(2,1)S(1)}, u32[]{:S(2)}, u32[]{:S(2)}) %collective-permute-start) | collective-permute-done | bytes 1146912 | tf_op jit(solution)/shard_map/ppermute | solution.py:348
  241.4 0.1 collective-permute-start.1
  241.4 1.4 put_late.1
  242.8 1.0 patch_own.1
  243.9 0.3 collective-permute-done.1.refs_2_
  244.2 1.0 patch_partner.1
Async XLA Ops:
  225.4 16.0 %collective-permute-start = (bf16[14,16,2560]{2,1,0:T(8,128)(2,1)S(1)}, bf16[14,16,2560]{2,1,0:T(8,128)(2,1)S(1)}, u32[]{:S(2)}, u32[]{:S(2)}) collective-permute-start(bf16[14,16,2560]{2,1,0:T(8,128)(2,1)S(1)} %get-tuple-element.42), channel_id=1, source_target_pairs={{0,6},{1,3},{2,0},{3,5},{4,2},{5,7},{6,4},{7,1},{8,14},{9,11},{10,... | collective-permute-start | bytes 3440648 | tf_op jit(solution)/shard_map/ppermute | solution.py:348
  241.4 2.8 %collective-permute-start.1 = (bf16[14,16,2560]{2,1,0:T(8,128)(2,1)S(1)}, bf16[14,16,2560]{2,1,0:T(8,128)(2,1)S(1)}, u32[]{:S(2)}, u32[]{:S(2)}) collective-permute-start(bf16[14,16,2560]{2,1,0:T(8,128)(2,1)S(1)} %collective-permute-done.refs_2_), channel_id=1, source_target_pairs={{0,1},{1,0},{2,3},{3,2},{4,5},{5,4},{6,7},{7,6},{8,9},{9,8},{10,11... | collective-permute-start | bytes 3440648 | tf_op jit(solution)/shard_map/ppermute | solution.py:352
